TPU v7x, 16 devices: a whole 2x2x2 slice. The times are simulated.
16 devices in a mesh: rep: 2 (over z), shard: 8 (over y, x, core).
Axes of the slice: x: 2, y: 2, z: 2, core: 2. Of those that a mesh axis runs over, the one named last changes fastest.
Arguments:
- x: bfloat16 [24576, 1536], P(('rep', 'shard'))
- seg_ids: int32 [24576], P(('rep', 'shard'))
- positions: int32 [24576], P(('rep', 'shard'))
- grad_y: bfloat16 [24576, 1536], P(('rep', 'shard'))
- num_tokens: int32 [1], replicated
- w_q: bfloat16 [1536, 1536], P('shard')
- b_q: bfloat16 [1536], P('shard')
- w_k: bfloat16 [1536, 256], P('shard')
- b_k: bfloat16 [256], P('shard')
- w_v: bfloat16 [1536, 256], P('shard')
- b_v: bfloat16 [256], P('shard')
- w_o: bfloat16 [1536, 1536], P('shard')
- w_gate: bfloat16 [1536, 8960], P('shard')
- w_up: bfloat16 [1536, 8960], P('shard')
- w_down: bfloat16 [8960, 1536], P('shard')
- norm_attn: bfloat16 [1536], P('shard')
- norm_mlp: bfloat16 [1536], P('shard')
Outputs:
- output 1: bfloat16 [24576, 1536], P(('rep', 'shard'))
- output 2: float32 [1536, 1536], P('shard')
- output 3: float32 [1536], P('shard')
- output 4: float32 [1536, 256], P('shard')
- output 5: float32 [256], P('shard')
- output 6: float32 [1536, 256], P('shard')
- output 7: float32 [256], P('shard')
- output 8: float32 [1536, 1536], P('shard')
- output 9: float32 [1536, 8960], P('shard')
- output 10: float32 [1536, 8960], P('shard')
- output 11: float32 [8960, 1536], P('shard')
- output 12: float32 [1536], P('shard')
- output 13: float32 [1536], P('shard')
All inputs are finite; a program needn't handle non-finite values.
Results may differ from a plain program's by a relative error of at most 0.02.
Values are sent between devices in bfloat16 or wider.
A program may use at most 1 GiB of HBM per device.

v0:
```python
import jax
import jax.numpy as jnp
import math
from jax import lax
from jax.sharding import PartitionSpec as P

HEAD_DIM = 128
ROPE_THETA = 1000000.0
EPS = 1e-6


def rope_tables(positions):
    half_dim = HEAD_DIM // 2
    inv_freq = ROPE_THETA ** (-2.0 * jnp.arange(half_dim, dtype=jnp.float32) / HEAD_DIM)
    angle = positions.astype(jnp.float32)[:, None] * inv_freq[None, :]
    cos_t = jnp.cos(angle)
    sin_t = jnp.sin(angle)
    return (jnp.concatenate([cos_t, cos_t], axis=-1)[:, None, :], jnp.concatenate([sin_t, sin_t], axis=-1)[:, None, :])


def rotate_half(vals):
    half_dim = vals.shape[-1] // 2
    return jnp.concatenate([-vals[..., half_dim:], vals[..., :half_dim]], axis=-1)


def rope_apply(vals, cos_t, sin_t):
    return vals * cos_t + rotate_half(vals) * sin_t


def rope_back(grads_in, cos_t, sin_t):
    return grads_in * cos_t - rotate_half(grads_in) * sin_t


def rms_inverse(vals):
    return lax.rsqrt(jnp.mean(vals * vals, axis=-1, keepdims=True) + EPS)


def rms_back(d_normed, vals, inv_rms, gain):
    d_scaled = d_normed * gain
    d_vals = inv_rms * d_scaled - vals * (inv_rms ** 3) * jnp.mean(d_scaled * vals, axis=-1, keepdims=True)
    return d_vals, jnp.sum(d_normed * vals * inv_rms, axis=0)


def round_bf(vals):
    return vals.astype(jnp.bfloat16).astype(jnp.float32)


def contract_rows(left, right):
    return lax.dot_general(left, right, (((0,), (0,)), ((), ())), preferred_element_type=jnp.float32)


def contract_cols(left, right):
    return lax.dot_general(left, right, (((1,), (1,)), ((), ())), preferred_element_type=jnp.float32)


def block_probs(q_blk, k_rot, row_ids, seg_rows, seg_ids):
    head_dim = q_blk.shape[-1]
    key_ids = jnp.arange(k_rot.shape[0])
    scores = jnp.einsum('qkgd,skd->kgqs', q_blk, k_rot, preferred_element_type=jnp.float32) * (head_dim ** -0.5)
    allowed = (seg_rows[:, None] == seg_ids[None, :]) & (row_ids[:, None] >= key_ids[None, :])
    return jax.nn.softmax(jnp.where(allowed, scores, -1e30), axis=-1)


def attention_fwd(q_rot, k_rot, v_all, seg_ids):
    tokens, kv_heads, group_size, head_dim = q_rot.shape
    q_rows = math.gcd(tokens, 256)
    n_blocks = tokens // q_rows

    def one_block(block_in):
        q_blk, row_ids, seg_rows = block_in
        prob_bf = block_probs(q_blk, k_rot, row_ids, seg_rows, seg_ids).astype(jnp.bfloat16)
        return jnp.einsum('kgqs,skd->qkgd', prob_bf, v_all, preferred_element_type=jnp.float32).astype(jnp.bfloat16)

    out_blocks = lax.map(one_block, (q_rot.reshape(n_blocks, q_rows, kv_heads, group_size, head_dim), jnp.arange(tokens).reshape(n_blocks, q_rows), seg_ids.reshape(n_blocks, q_rows)))
    return out_blocks.reshape(tokens, kv_heads * group_size * head_dim)


def attention_bwd(q_rot, k_rot, v_all, d_out, seg_ids):
    tokens, kv_heads, group_size, head_dim = q_rot.shape
    q_rows = math.gcd(tokens, 256)
    n_blocks = tokens // q_rows
    scale = head_dim ** -0.5

    def one_block(carry_in, block_in):
        key_acc, val_acc = carry_in
        q_blk, dout_blk, row_ids, seg_rows = block_in
        prob_f = block_probs(q_blk, k_rot, row_ids, seg_rows, seg_ids)
        prob_bf = prob_f.astype(jnp.bfloat16)
        val_acc = val_acc + jnp.einsum('kgqs,qkgd->skd', prob_bf, dout_blk, preferred_element_type=jnp.float32)
        d_prob = jnp.einsum('qkgd,skd->kgqs', dout_blk, v_all, preferred_element_type=jnp.float32)
        d_score = prob_f * (d_prob - jnp.sum(prob_f * d_prob, axis=-1, keepdims=True))
        d_score_bf = (d_score * scale).astype(jnp.bfloat16)
        key_acc = key_acc + jnp.einsum('kgqs,qkgd->skd', d_score_bf, q_blk, preferred_element_type=jnp.float32)
        d_query = jnp.einsum('kgqs,skd->qkgd', d_score_bf, k_rot, preferred_element_type=jnp.float32)
        return (key_acc, val_acc), d_query

    zero_acc = jnp.zeros(k_rot.shape, jnp.float32)
    block_shape = (n_blocks, q_rows, kv_heads, group_size, head_dim)
    (d_key, d_val), d_query = lax.scan(one_block, (zero_acc, zero_acc), (q_rot.reshape(block_shape), d_out.reshape(block_shape), jnp.arange(tokens).reshape(n_blocks, q_rows), seg_ids.reshape(n_blocks, q_rows)))
    return d_query.reshape(tokens, kv_heads, group_size, head_dim), d_key, d_val


def local_layer(x, seg_ids, positions, grad_y, weights):
    (w_q, b_q, w_k, b_k, w_v, b_v, w_o, w_gate, w_up, w_down, norm_attn, norm_mlp) = weights
    tokens = x.shape[0]
    q_heads = w_q.shape[1] // HEAD_DIM
    kv_heads = w_k.shape[1] // HEAD_DIM
    group_size = q_heads // kv_heads
    cos_t, sin_t = rope_tables(positions)
    x_f = x.astype(jnp.float32)
    gain_in = norm_attn.astype(jnp.float32)
    gain_mid = norm_mlp.astype(jnp.float32)
    inv_in = rms_inverse(x_f)
    normed_in = (x_f * inv_in * gain_in).astype(jnp.bfloat16)
    q_lin = jnp.dot(normed_in, w_q, preferred_element_type=jnp.float32) + b_q.astype(jnp.float32)
    k_lin = jnp.dot(normed_in, w_k, preferred_element_type=jnp.float32) + b_k.astype(jnp.float32)
    v_lin = jnp.dot(normed_in, w_v, preferred_element_type=jnp.float32) + b_v.astype(jnp.float32)
    q_rot = rope_apply(q_lin.reshape(tokens, q_heads, HEAD_DIM), cos_t, sin_t).astype(jnp.bfloat16).reshape(tokens, kv_heads, group_size, HEAD_DIM)
    k_rot = rope_apply(k_lin.reshape(tokens, kv_heads, HEAD_DIM), cos_t, sin_t).astype(jnp.bfloat16)
    v_all = v_lin.astype(jnp.bfloat16).reshape(tokens, kv_heads, HEAD_DIM)
    attn_out = attention_fwd(q_rot, k_rot, v_all, seg_ids)
    resid_f = round_bf(x_f + jnp.dot(attn_out, w_o, preferred_element_type=jnp.float32))
    inv_mid = rms_inverse(resid_f)
    normed_mid = (resid_f * inv_mid * gain_mid).astype(jnp.bfloat16)
    gate_pre = jnp.dot(normed_mid, w_gate, preferred_element_type=jnp.float32)
    up_proj = jnp.dot(normed_mid, w_up, preferred_element_type=jnp.float32)
    sig_gate = jax.nn.sigmoid(gate_pre)
    act_gate = gate_pre * sig_gate
    hidden = (act_gate * up_proj).astype(jnp.bfloat16)

    grad_w_down = contract_rows(hidden, grad_y)
    d_hidden = round_bf(contract_cols(grad_y, w_down))
    d_gate = (d_hidden * up_proj * sig_gate * (1.0 + gate_pre * (1.0 - sig_gate))).astype(jnp.bfloat16)
    d_up = (d_hidden * act_gate).astype(jnp.bfloat16)
    grad_w_gate = contract_rows(normed_mid, d_gate)
    grad_w_up = contract_rows(normed_mid, d_up)
    d_normed_mid = round_bf(contract_cols(d_gate, w_gate) + contract_cols(d_up, w_up))
    d_resid_norm, grad_norm_mlp = rms_back(d_normed_mid, resid_f, inv_mid, gain_mid)
    d_resid = (grad_y.astype(jnp.float32) + d_resid_norm).astype(jnp.bfloat16)
    grad_w_o = contract_rows(attn_out, d_resid)
    d_attn = contract_cols(d_resid, w_o).astype(jnp.bfloat16).reshape(tokens, kv_heads, group_size, HEAD_DIM)
    d_query, d_key, d_val = attention_bwd(q_rot, k_rot, v_all, d_attn, seg_ids)
    d_q_lin = rope_back(round_bf(d_query).reshape(tokens, q_heads, HEAD_DIM), cos_t, sin_t).reshape(tokens, q_heads * HEAD_DIM)
    d_k_lin = rope_back(round_bf(d_key), cos_t, sin_t).reshape(tokens, kv_heads * HEAD_DIM)
    d_v_lin = round_bf(d_val).reshape(tokens, kv_heads * HEAD_DIM)
    d_q_bf = d_q_lin.astype(jnp.bfloat16)
    d_k_bf = d_k_lin.astype(jnp.bfloat16)
    d_v_bf = d_v_lin.astype(jnp.bfloat16)
    grad_w_q = contract_rows(normed_in, d_q_bf)
    grad_w_k = contract_rows(normed_in, d_k_bf)
    grad_w_v = contract_rows(normed_in, d_v_bf)
    d_normed_in = round_bf(contract_cols(d_q_bf, w_q) + contract_cols(d_k_bf, w_k) + contract_cols(d_v_bf, w_v))
    d_x_norm, grad_norm_attn = rms_back(d_normed_in, x_f, inv_in, gain_in)
    grad_x = (d_resid.astype(jnp.float32) + d_x_norm).astype(jnp.bfloat16)
    return grad_x, (grad_w_q, jnp.sum(d_q_lin, axis=0), grad_w_k, jnp.sum(d_k_lin, axis=0), grad_w_v, jnp.sum(d_v_lin, axis=0), grad_w_o, grad_w_gate, grad_w_up, grad_w_down, grad_norm_attn, grad_norm_mlp)


def solution(mesh):
    batch_spec = P(('rep', 'shard'), None)
    row_spec = P(('rep', 'shard'))
    mat_spec = P('shard', None)
    vec_spec = P('shard')
    weight_specs = (mat_spec, vec_spec, mat_spec, vec_spec, mat_spec, vec_spec, mat_spec, mat_spec, mat_spec, mat_spec, vec_spec, vec_spec)
    in_specs = (batch_spec, row_spec, row_spec, batch_spec, P(None)) + weight_specs
    out_specs = (batch_spec,) + weight_specs

    def per_device(x, seg_ids, positions, grad_y, num_tokens, w_q, b_q, w_k, b_k, w_v, b_v, w_o, w_gate, w_up, w_down, norm_attn, norm_mlp):
        shards = (w_q, b_q, w_k, b_k, w_v, b_v, w_o, w_gate, w_up, w_down, norm_attn, norm_mlp)
        gathered = tuple(lax.all_gather(part_w, 'shard', axis=0, tiled=True) for part_w in shards)
        grad_x, grad_list = local_layer(x, seg_ids, positions, grad_y, gathered)
        inv_count = 1.0 / num_tokens[0].astype(jnp.float32)
        reduced = tuple(lax.psum(lax.psum_scatter(full_grad, 'shard', scatter_dimension=0, tiled=True), 'rep') * inv_count for full_grad in grad_list)
        return (grad_x,) + reduced

    return jax.shard_map(per_device, mesh=mesh, in_specs=in_specs, out_specs=out_specs, check_vma=False)
```

profile of v0, /device:TPU:0, one launch (start us, length us, event | category | flops | bytes accessed | tf_op | source)
XLA Modules:
  0.0 3013.8 jit_solution(8217176611007321965)
XLA Ops:
  13.9 26.8 all-reduce.13
  200.8 14.2 fusion.109
  218.5 137.7 %while.25 = (s32[]{:T(128)}, bf16[6,256,2,6,128]{4,1,3,2,0:T(8,128)(2,1)}, s32[6,256]{1,0:T(8,128)S(1)}, s32[1536]{0:T(1024)S(1)}, s32[6,256]{1,0:T(8,128)S(1)},...) while((s32[]{:T(128)}, ...), condition=%wide.region_4.5_spmd, body=%wide.region_1.4_spmd.sunk | while | flops 2445805056 | bytes 41718880 | solution.py:74
  390.5 52.7 %fusion.151 = f32[1536,8960]{1,0:T(8,128)} fusion(bf16[1536,8960]{1,0:T(8,128)(2,1)} %all-gather.12.cloned.1.call-done, bf16[1536,1536]{0,1:T(8,128)(2,1)} %get-tuple-element.347, f32[1536]{0:T(1024)S(1)} %copy-done.49, f32[1536]{0:T(1024)S(1)} %get-tuple-element.343), kind=kOutput, calls=%fused_computation.200 | convolution fusion | flops 42288021504 | bytes 87306240 | tf_op jit(solution)/shard_map/dot_general | solution.py:126
  443.3 52.9 %fusion.149 = f32[1536,8960]{1,0:T(8,128)} fusion(bf16[1536,8960]{1,0:T(8,128)(2,1)} %all-gather.14.cloned.1.call-done, bf16[1536,1536]{0,1:T(8,128)(2,1)} %get-tuple-element.347, f32[1536]{0:T(1024)S(1)} %copy-done.49, f32[1536]{0:T(1024)S(1)} %get-tuple-element.343), kind=kOutput, calls=%fused_computation.199 | convolution fusion | flops 42288021504 | bytes 87306240 | tf_op jit(solution)/shard_map/dot_general | solution.py:125
  496.1 75.4 %fusion.105 = (bf16[1536,8960]{1,0:T(8,128)(2,1)}, bf16[1536,8960]{1,0:T(8,128)(2,1)}) fusion(f32[1536,8960]{1,0:T(8,128)} %fusion.149, f32[1536,8960]{1,0:T(8,128)} %fusion.151, bf16[1536,1536]{1,0:T(8,128)(2,1)} %param.24, bf16[8960,1536]{1,0:T(8,128)(2,1)} %all-gather.10.cloned.1.call-done), kind=kOutput, calls=%fused_computation.94 | convolution fusion | flops 42485022720 | bytes 197394432 | tf_op jit(solution)/shard_map/dot_general | solution.py:53
  571.6 52.5 %fusion.172 = f32[1536,1536]{0,1:T(8,128)} fusion(bf16[1536,8960]{1,0:T(8,128)(2,1)} %get-tuple-element.325, bf16[1536,8960]{1,0:T(8,128)(2,1)} %all-gather.14.cloned.1.call-done), kind=kOutput, calls=%fused_computation.204 | convolution fusion | flops 42278584320 | bytes 64487424 | tf_op jit(solution)/shard_map/dot_general | solution.py:53
  624.0 57.8 %fusion.126 = (f32[1536]{0:T(1024)}, f32[1536]{0:T(1024)S(1)}, bf16[1536,1536]{0,1:T(8,128)(2,1)}) fusion(bf16[1536,1536]{0,1:T(8,128)(2,1)} %get-tuple-element.347, f32[1536]{0:T(1024)S(1)} %copy-done.46, f32[1536]{0:T(1024)S(1)} %copy-done.50, f32[1536,1536]{0,1:T(8,128)} %fusion.172, bf16[1536,8960]{1,0:T(8,128)(2,1)} %get-tuple-element.324, ...), kind=kOutput, calls=%fused_computation.136 | convolution fusion | flops 42302177280 | bytes 73949184 | tf_op jit(solution)/shard_map/dot_general | solution.py:53
  717.8 544.0 %while.26 = (s32[]{:T(128)}, f32[1536,2,128]{0,2,1:T(8,128)S(1)}, f32[1536,2,128]{0,2,1:T(8,128)}, bf16[6,256,2,6,128]{4,1,3,2,0:T(8,128)(2,1)}, bf16[6,256,2,6,...) while((s32[]{:T(128)}, f32[1536,2,128]{0,2,1:T(8,128)S(1)}, ...), condition=%wide.region_11.12_spmd.clone, body=%wide.region_7.11_spmd.clone.sunk | while | flops 6136932864 | bytes 221928112 | solution.py:99
  740.5 28.7 bitcast_dynamic-update-slice_fusion.2
  778.7 29.6 fusion.256
  830.8 28.7 bitcast_dynamic-update-slice_fusion.2
  869.4 29.4 fusion.256
  921.4 28.7 bitcast_dynamic-update-slice_fusion.2
  960.0 29.5 fusion.256
  1012.0 28.7 bitcast_dynamic-update-slice_fusion.2
  1050.6 29.5 fusion.256
  1102.7 28.7 bitcast_dynamic-update-slice_fusion.2
  1141.3 29.5 fusion.256
  1193.4 28.7 bitcast_dynamic-update-slice_fusion.2
  1232.0 29.4 fusion.256
  1296.8 14.5 slice_negate_fusion
  1388.6 52.3 %fusion.145 = f32[1536,8960]{1,0:T(8,128)} fusion(bf16[1536,8960]{1,0:T(8,128)(2,1)} %get-tuple-element.324, bf16[1536,1536]{0,1:T(8,128)(2,1)} %get-tuple-element.347, f32[1536]{0:T(1024)S(1)} %copy-done.51, f32[1536]{0:T(1024)S(1)} %copy-done.47), kind=kOutput, calls=%fused_computation.197 | convolution fusion | flops 42288021504 | bytes 87306240 | tf_op jit(solution)/shard_map/dot_general | solution.py:49
  1441.0 52.0 %fusion.147 = f32[1536,8960]{1,0:T(8,128)} fusion(bf16[1536,8960]{1,0:T(8,128)(2,1)} %get-tuple-element.325, bf16[1536,1536]{0,1:T(8,128)(2,1)} %get-tuple-element.347, f32[1536]{0:T(1024)S(1)} %copy-done.51, f32[1536]{0:T(1024)S(1)} %copy-done.47), kind=kOutput, calls=%fused_computation.198 | convolution fusion | flops 42288021504 | bytes 87306240 | tf_op jit(solution)/shard_map/dot_general | solution.py:49
  1493.0 73.9 %fusion.107 = f32[8960,1536]{1,0:T(8,128)} fusion(bf16[1536,1536]{1,0:T(8,128)(2,1)} %param.24, f32[1536,8960]{1,0:T(8,128)} %fusion.151, f32[1536,8960]{1,0:T(8,128)} %fusion.149), kind=kOutput, calls=%fused_computation.99 | convolution fusion | flops 42361159680 | bytes 169869312 | tf_op jit(solution)/shard_map/dot_general | solution.py:49
  1567.3 276.9 %reduce-scatter.18.cloned.1.call-done = f32[192,8960]{1,0:T(8,128)} async-done(((f32[1536,8960]{1,0:T(8,128)}), f32[192,8960]{1,0:T(8,128)}) %reduce-scatter.18.cloned.1.call-update) | async-done | bytes 6881296 | tf_op jit(solution)/shard_map/reduce_scatter | solution.py:172
  1844.2 311.9 %reduce-scatter.16.cloned.1.call-done = f32[192,8960]{1,0:T(8,128)} async-done(((f32[1536,8960]{1,0:T(8,128)}), f32[192,8960]{1,0:T(8,128)}) %reduce-scatter.16.cloned.1.call-update) | async-done | bytes 6881296 | tf_op jit(solution)/shard_map/reduce_scatter | solution.py:172
  2156.1 311.7 %reduce-scatter.20.cloned.1.call-done = f32[1120,1536]{1,0:T(8,128)} async-done(((f32[8960,1536]{1,0:T(8,128)}), f32[1120,1536]{1,0:T(8,128)}) %reduce-scatter.20.cloned.1.call-update) | async-done | bytes 6881296 | tf_op jit(solution)/shard_map/reduce_scatter | solution.py:172
  2469.9 13.9 copy.107
  2483.8 13.9 copy.108
  2527.6 23.3 all-reduce.10
  2575.5 412.2 %all-reduce.16.cloned.1.call-done = (f32[192,1536]{1,0:T(8,128)}, f32[192,256]{1,0:T(8,128)}, f32[192,256]{1,0:T(8,128)}, f32[192,1536]{1,0:T(8,128)}, f32[192,8...) async-done(((f32[192,1536]{1,0:T(8,128)}, f32[192,256]{1,0:T(8,128)}, f32[192,256]{1,0:T(8,128)}, f32[192,1536]{1,0:T(8,128)}, f32[192,8960]{1,0:T(8,128)}, ...) | async-done | bytes 23396368 | tf_op jit(solution)/shard_map/psum | solution.py:172
  (356 shorter events, 756.7 us)
Async XLA Ops:
  7.2 116.8 %all-gather.6.cloned.1.call-start = ((), (), s32[]{:S(2)}) async-start(), calls=%async_computation.7 | async-start | bytes 5308416 | tf_op jit(solution)/shard_map/all_gather | solution.py:169
  8.0 368.4 %all-gather.8.cloned.1.call-start = ((), (), s32[]{:S(2)}) async-start(), calls=%async_computation.8 | async-start | bytes 5308416 | tf_op jit(solution)/shard_map/all_gather | solution.py:169
  8.7 381.8 %all-gather.12.cloned.1.call-start = ((), (), s32[]{:S(2)}) async-start(), calls=%async_computation.10 | async-start | bytes 30965760 | tf_op jit(solution)/shard_map/all_gather | solution.py:169
  9.5 433.8 %all-gather.14.cloned.1.call-start = ((), (), s32[]{:S(2)}) async-start(), calls=%async_computation.11 | async-start | bytes 30965760 | tf_op jit(solution)/shard_map/all_gather | solution.py:169
  10.0 41.3 %copy-start.36 = (bf16[192,256]{1,0:T(8,128)(2,1)S(1)}, bf16[192,256]{1,0:T(8,128)(2,1)}, u32[]{:S(2)}) copy-start(bf16[192,256]{1,0:T(8,128)(2,1)} %param.28) | copy-start | bytes 294916
  10.0 486.1 %all-gather.10.cloned.1.call-start = ((), (), s32[]{:S(2)}) async-start(), calls=%async_computation.9 | async-start | bytes 30965760 | tf_op jit(solution)/shard_map/all_gather | solution.py:169
  10.6 1556.6 %reduce-scatter.10.cloned.1.call-start = ((), (), s32[]{:S(2)}) async-start(), calls=%async_computation.13 | async-start | bytes 1769472 | tf_op jit(solution)/shard_map/reduce_scatter | solution.py:172
  40.7 25.8 copy-start.40
  71.6 27.1 copy-start.7
  71.6 36.3 %copy-start.5 = (f32[1536,128]{0,1:T(8,128)}, f32[1536,128]{0,1:T(8,128)S(1)}, u32[]{:S(2)}) copy-start(f32[1536,128]{0,1:T(8,128)S(1)} %get-tuple-element.352) | copy-start | bytes 2359300
  75.7 24.6 copy-start.26
  124.0 76.7 %copy-start.9 = (f32[6,256,128]{2,1,0:T(8,128)}, f32[6,256,128]{2,1,0:T(8,128)S(1)}, u32[]{:S(2)}) copy-start(f32[6,256,128]{2,1,0:T(8,128)S(1)} %get-tuple-element.350) | copy-start | bytes 2359300
  124.0 76.7 %copy-start.11 = (f32[6,256,128]{2,1,0:T(8,128)}, f32[6,256,128]{2,1,0:T(8,128)S(1)}, u32[]{:S(2)}) copy-start(f32[6,256,128]{2,1,0:T(8,128)S(1)} %get-tuple-element.351) | copy-start | bytes 2359300
  356.2 20.1 copy-start.2
  356.2 20.1 copy-start.42
  356.2 20.1 copy-start.43
  390.5 52.8 %copy-start.45 = (f32[1536]{0:T(1024)}, f32[1536]{0:T(1024)S(1)}, u32[]{:S(2)}) copy-start(f32[1536]{0:T(1024)S(1)} %get-tuple-element.343) | copy-start | bytes 18436
  571.6 52.5 %copy-start.46 = (f32[1536]{0:T(1024)S(1)}, f32[1536]{0:T(1024)}, u32[]{:S(2)}) copy-start(f32[1536]{0:T(1024)} %copy-done.45) | copy-start | bytes 18436
  571.6 52.5 %copy-start.50 = (f32[1536]{0:T(1024)S(1)}, f32[1536]{0:T(1024)}, u32[]{:S(2)}) copy-start(f32[1536]{0:T(1024)} %convert_element_type.170) | copy-start | bytes 18436
  624.0 57.8 %copy-start.48 = (f32[1536]{0:T(1024)S(1)}, f32[1536]{0:T(1024)}, u32[]{:S(2)}) copy-start(f32[1536]{0:T(1024)} %get-tuple-element.342) | copy-start | bytes 18436
  700.9 16.9 copy-start.27
  700.9 16.9 copy-start.31
  1296.7 270.5 %reduce-scatter.12.cloned.1.call-start = ((), (), s32[]{:S(2)}) async-start(), calls=%async_computation.14 | async-start | bytes 1769472 | tf_op jit(solution)/shard_map/reduce_scatter | solution.py:172
  1349.9 217.4 %reduce-scatter.8.cloned.1.call-start = ((), (), s32[]{:S(2)}) async-start(), calls=%async_computation.12 | async-start | bytes 10616832 | tf_op jit(solution)/shard_map/reduce_scatter | solution.py:172
  1374.5 192.8 %reduce-scatter.14.cloned.1.call-start = ((), (), s32[]{:S(2)}) async-start(), calls=%async_computation.15 | async-start | bytes 10616832 | tf_op jit(solution)/shard_map/reduce_scatter | solution.py:172
  1387.9 456.3 %reduce-scatter.18.cloned.1.call-start = ((), (), s32[]{:S(2)}) async-start(), calls=%async_computation.17 | async-start | bytes 61931520 | tf_op jit(solution)/shard_map/reduce_scatter | solution.py:172
  1440.9 715.2 %reduce-scatter.16.cloned.1.call-start = ((), (), s32[]{:S(2)}) async-start(), calls=%async_computation.16 | async-start | bytes 61931520 | tf_op jit(solution)/shard_map/reduce_scatter | solution.py:172
  1493.0 974.9 %reduce-scatter.20.cloned.1.call-start = ((), (), s32[]{:S(2)}) async-start(), calls=%async_computation.18 | async-start | bytes 61931520 | tf_op jit(solution)/shard_map/reduce_scatter | solution.py:172
  1567.0 1420.7 %all-reduce.16.cloned.1.call-start = ((), (), s32[]{:S(2)}) async-start(), calls=%async_computation.19 | async-start | bytes 46792704 | tf_op jit(solution)/shard_map/psum | solution.py:172
  2469.9 27.9 slice-start.2
  2497.8 24.8 slice-start
  2522.7 28.6 copy-start.44
  (60 other events, 434.6 us)
Sparse Core Ops, SparseCore 0:
  9.9 38.0 all-gather.5
  49.8 36.0 all-gather.7
  87.8 131.4 all-gather.11
  220.9 131.4 all-gather.13
  354.0 131.4 all-gather.9
  1296.9 32.9 reduce-scatter.9
  1350.0 33.0 reduce-scatter.11
  1386.6 71.2 reduce-scatter.7
  1461.3 71.2 reduce-scatter.13
  1536.0 308.2 reduce-scatter.17
  1847.8 308.2 reduce-scatter.15
  2159.6 308.2 reduce-scatter.19
  2471.1 516.5 all-reduce.15
where the time goes:
time: 3030 us; the launch traced here: 3010 us
  waiting for transfers between devices  1320 us (44%)
  matrix products  1230 us (41%)
  local copies, waits for them, and re-layouts  226 us (7%)
  other arithmetic  143 us (5%)
  blocking collectives  77.2 us (3%)
    reduce_scatter x7, waiting for transfers between devices, per_device(): lax.psum_scatter(full_grad, 'shard', scatter_dimension=0, tiled=True)  901 us
    psum x1, waiting for transfers between devices, per_device(): lax.psum(lax.psum_scatter(full_grad, 'shard', scatter_dimension=0, tiled=...  412 us
    dot_general x7, matrix products, contract_cols(): lax.dot_general(left, right, (((1,), (1,)), ((), ())), preferred_element_...  212 us
    dot_general x7, matrix products, contract_rows(): lax.dot_general(left, right, (((0,), (0,)), ((), ())), preferred_element_...  211 us
    dot_general x6, matrix products, one_block(): jnp.einsum('kgqs,qkgd->skd', d_score_bf, q_blk, preferred_element_type=jn...  177 us
    dot_general x6, matrix products, one_block(): jnp.einsum('kgqs,skd->qkgd', d_score_bf, k_rot, preferred_element_type=jn...  172 us
    sub x12, matrix products, block_probs(): return jax.nn.softmax(jnp.where(allowed, scores, -1e+30), axis=-1)  144 us
    dot_general x6, matrix products, one_block(): jnp.einsum('kgqs,skd->qkgd', prob_bf, v_all, preferred_element_type=jnp.f...  62 us
  transfers between devices with their start and end apart: 13, of which 4 were waited for; matrix products, arithmetic and copies ran while one was open for 26% of the time, Pallas kernels for 0%

commit v1 on v0

v1 whole, which is shorter than its diff:
```python
import jax
import jax.numpy as jnp
from jax import lax
from jax.experimental import pallas as pl
from jax.experimental.pallas import tpu as pltpu
from jax.sharding import PartitionSpec as P


HEAD_DIM = 128
HEADS = 12
KV_HEADS = 2
GROUP = HEADS // KV_HEADS
ROPE_THETA = 1000000.0
EPS = 1e-6
QB = 256
SCALE = HEAD_DIM ** -0.5


def rope_tables(positions):
    half_dim = HEAD_DIM // 2
    inv_freq = ROPE_THETA ** (-2.0 * jnp.arange(half_dim, dtype=jnp.float32) / HEAD_DIM)
    angle = positions.astype(jnp.float32)[:, None] * inv_freq[None, :]
    cos_t = jnp.cos(angle)
    sin_t = jnp.sin(angle)
    return jnp.concatenate([cos_t, cos_t], axis=-1), jnp.concatenate([-sin_t, sin_t], axis=-1)


def dot_nn(a, b):
    return lax.dot_general(a, b, (((1,), (0,)), ((), ())), preferred_element_type=jnp.float32)


def dot_nt(a, b):
    return lax.dot_general(a, b, (((1,), (1,)), ((), ())), preferred_element_type=jnp.float32)


def dot_tn(a, b):
    return lax.dot_general(a, b, (((0,), (0,)), ((), ())), preferred_element_type=jnp.float32)


def round_bf(vals):
    return lax.reduce_precision(vals, 8, 7)


def masked_scores(k_part, q_blk, first_row, start_row):
    s_t = dot_nt(k_part, q_blk) * SCALE
    key_idx = lax.broadcasted_iota(jnp.int32, s_t.shape, 0)
    row_idx = lax.broadcasted_iota(jnp.int32, s_t.shape, 1) + first_row
    return jnp.where((key_idx >= start_row) & (key_idx <= row_idx), s_t, -1e30)


def attn_fwd_kernel(q_in, k_in, v_in, cos_ref, sin_ref, start_ref, q_out, k_out, v_out, o_out, vt_scr):
    tokens = q_in.shape[0]

    @pl.when(pl.program_id(0) % GROUP == 0)
    def _():
        k_f = k_in[...]
        k_out[...] = (k_f * cos_ref[...] + pltpu.roll(k_f, HEAD_DIM // 2, 1) * sin_ref[...]).astype(jnp.bfloat16)
        v_f = v_in[...]
        v_out[...] = v_f.astype(jnp.bfloat16)
        vt_scr[...] = v_f.T.astype(jnp.bfloat16)

    q_f = q_in[...]
    q_out[...] = (q_f * cos_ref[...] + pltpu.roll(q_f, HEAD_DIM // 2, 1) * sin_ref[...]).astype(jnp.bfloat16)
    for first in range(0, tokens, QB):
        keys = first + QB
        s_t = masked_scores(k_out[:keys, :], q_out[first:keys, :], first, start_ref[0:1, first:keys])
        e_t = jnp.exp(s_t - jnp.max(s_t, axis=0, keepdims=True))
        p_t = (e_t / jnp.sum(e_t, axis=0, keepdims=True)).astype(jnp.bfloat16)
        o_t = dot_nn(vt_scr[:, :keys], p_t)
        o_out[first:keys, :] = o_t.T.astype(jnp.bfloat16)


def column_sums(vals):
    return jnp.broadcast_to(jnp.sum(vals, axis=0, keepdims=True), (8, vals.shape[1]))


def attn_bwd_kernel(q_ref, k_ref, v_ref, do_ref, cos_ref, sin_ref, start_ref, dq_out, dk_out, dv_out, bq_out, bk_out, bv_out, dk_acc, dv_acc, kt_scr, dq_scr):
    tokens = q_ref.shape[0]
    step = pl.program_id(0) % GROUP

    @pl.when(step == 0)
    def _():
        kt_scr[...] = k_ref[...].astype(jnp.float32).T.astype(jnp.bfloat16)
        dk_acc[...] = jnp.zeros_like(dk_acc)
        dv_acc[...] = jnp.zeros_like(dv_acc)

    for first in range(0, tokens, QB):
        keys = first + QB
        q_blk = q_ref[first:keys, :]
        do_blk = do_ref[first:keys, :]
        s_t = masked_scores(k_ref[:keys, :], q_blk, first, start_ref[0:1, first:keys])
        e_t = jnp.exp(s_t - jnp.max(s_t, axis=0, keepdims=True))
        p_t = e_t / jnp.sum(e_t, axis=0, keepdims=True)
        dp_t = dot_nt(v_ref[:keys, :], do_blk)
        dv_acc[:keys, :] += dot_nn(p_t.astype(jnp.bfloat16), do_blk)
        delta = jnp.sum(p_t * dp_t, axis=0, keepdims=True)
        ds_t = (p_t * (dp_t - delta) * SCALE).astype(jnp.bfloat16)
        dk_acc[:keys, :] += dot_nn(ds_t, q_blk)
        dq_scr[first:keys, :] = dot_nn(kt_scr[:, :keys], ds_t).T

    def rope_back(grad):
        grad = grad.astype(jnp.bfloat16).astype(jnp.float32)
        return grad * cos_ref[...] - pltpu.roll(grad, HEAD_DIM // 2, 1) * sin_ref[...]

    dq_lin = rope_back(dq_scr[...])
    dq_out[...] = dq_lin.astype(jnp.bfloat16)
    bq_out[...] = column_sums(dq_lin)

    @pl.when(step == GROUP - 1)
    def _():
        dk_lin = rope_back(dk_acc[...])
        dk_out[...] = dk_lin.astype(jnp.bfloat16)
        bk_out[...] = column_sums(dk_lin)
        dv_bf = dv_acc[...].astype(jnp.bfloat16)
        dv_out[...] = dv_bf
        bv_out[...] = column_sums(dv_bf.astype(jnp.float32))


def head_spec(tokens, base):
    return pl.BlockSpec((tokens, HEAD_DIM), lambda h: (0, base + h))


def kv_spec(tokens, base):
    return pl.BlockSpec((tokens, HEAD_DIM), lambda h: (0, base + h // GROUP))


def whole_spec(shape):
    return pl.BlockSpec(shape, lambda h: (0, 0))


def attention_fwd(qkv_lin, cos_t, sin_t, start_row):
    tokens = qkv_lin.shape[0]
    table = whole_spec((tokens, HEAD_DIM))
    pairs = HEADS * tokens * tokens * 0.6
    return pl.pallas_call(
        attn_fwd_kernel,
        grid=(HEADS,),
        in_specs=[head_spec(tokens, 0), kv_spec(tokens, HEADS), kv_spec(tokens, HEADS + KV_HEADS), table, table, whole_spec((8, tokens))],
        out_specs=[head_spec(tokens, 0), kv_spec(tokens, 0), kv_spec(tokens, 0), head_spec(tokens, 0)],
        out_shape=[
            jax.ShapeDtypeStruct((tokens, HEADS * HEAD_DIM), jnp.bfloat16),
            jax.ShapeDtypeStruct((tokens, KV_HEADS * HEAD_DIM), jnp.bfloat16),
            jax.ShapeDtypeStruct((tokens, KV_HEADS * HEAD_DIM), jnp.bfloat16),
            jax.ShapeDtypeStruct((tokens, HEADS * HEAD_DIM), jnp.bfloat16),
        ],
        scratch_shapes=[pltpu.VMEM((HEAD_DIM, tokens), jnp.bfloat16)],
        compiler_params=pltpu.CompilerParams(dimension_semantics=("arbitrary",), vmem_limit_bytes=48 * 1024 * 1024),
        cost_estimate=pl.CostEstimate(flops=int(pairs * 128 * 16), bytes_accessed=30000000, transcendentals=int(pairs)),
        name="attn_fwd",
    )(qkv_lin, qkv_lin, qkv_lin, cos_t, sin_t, start_row)


def attention_bwd(q_rot, k_rot, v_all, d_out, cos_t, sin_t, start_row):
    tokens = q_rot.shape[0]
    table = whole_spec((tokens, HEAD_DIM))
    pairs = HEADS * tokens * tokens * 0.6
    row_q = pl.BlockSpec((8, HEAD_DIM), lambda h: (0, h))
    row_kv = pl.BlockSpec((8, HEAD_DIM), lambda h: (0, h // GROUP))
    acc = pltpu.VMEM((tokens, HEAD_DIM), jnp.float32)
    q_cols = HEADS * HEAD_DIM
    kv_cols = KV_HEADS * HEAD_DIM
    return pl.pallas_call(
        attn_bwd_kernel,
        grid=(HEADS,),
        in_specs=[head_spec(tokens, 0), kv_spec(tokens, 0), kv_spec(tokens, 0), head_spec(tokens, 0), table, table, whole_spec((8, tokens))],
        out_specs=[head_spec(tokens, 0), kv_spec(tokens, 0), kv_spec(tokens, 0), row_q, row_kv, row_kv],
        out_shape=[
            jax.ShapeDtypeStruct((tokens, q_cols), jnp.bfloat16),
            jax.ShapeDtypeStruct((tokens, kv_cols), jnp.bfloat16),
            jax.ShapeDtypeStruct((tokens, kv_cols), jnp.bfloat16),
            jax.ShapeDtypeStruct((8, q_cols), jnp.float32),
            jax.ShapeDtypeStruct((8, kv_cols), jnp.float32),
            jax.ShapeDtypeStruct((8, kv_cols), jnp.float32),
        ],
        scratch_shapes=[acc, acc, pltpu.VMEM((HEAD_DIM, tokens), jnp.bfloat16), acc],
        compiler_params=pltpu.CompilerParams(dimension_semantics=("arbitrary",), vmem_limit_bytes=48 * 1024 * 1024),
        cost_estimate=pl.CostEstimate(flops=int(pairs * 128 * 30), bytes_accessed=30000000, transcendentals=int(pairs)),
        name="attn_bwd",
    )(q_rot, k_rot, v_all, d_out, cos_t, sin_t, start_row)


def rms_inverse(vals):
    return lax.rsqrt(jnp.mean(vals * vals, axis=-1, keepdims=True) + EPS)


def rms_back(d_normed, vals, inv_rms, gain):
    d_scaled = d_normed * gain
    d_vals = inv_rms * d_scaled - vals * (inv_rms ** 3) * jnp.mean(d_scaled * vals, axis=-1, keepdims=True)
    return d_vals, jnp.sum(d_normed * vals * inv_rms, axis=0)


def pick(arr, index, axis):
    return lax.dynamic_index_in_dim(arr, index, axis, keepdims=False)


def swap(arr, bit):
    return lax.ppermute(arr, 'shard', [(s, s ^ bit) for s in range(8)])


def swap_rep(arr):
    return lax.ppermute(arr, 'rep', [(0, 1), (1, 0)])


def f32(arr):
    return arr.astype(jnp.float32)


def bf16(arr):
    return arr.astype(jnp.bfloat16)


def stack_rows(vecs):
    rows = [jnp.pad(v, [(0, 0)] * (v.ndim - 1) + [(0, 256 - v.shape[-1])]) for v in vecs]
    rows = jnp.concatenate(rows, axis=-2)
    return jnp.pad(rows, [(0, 0)] * (rows.ndim - 2) + [(0, 8 - len(vecs)), (0, 0)])


class Spot:
    def __init__(self):
        shard = lax.axis_index('shard')
        self.core = shard % 2
        self.x = (shard // 2) % 2
        self.y = shard // 4


def split_rows(spot, acts, rows):
    tokens = acts.shape[0]
    cut = acts.T.reshape(2, 2, 2, rows, tokens)
    to_core = pick(cut, 1 - spot.core, 2).reshape(4 * rows, tokens)
    mine = pick(cut, spot.core, 2)
    x_send = pick(mine, 1 - spot.x, 1).reshape(2 * rows, tokens)
    x_keep = pick(mine, spot.x, 1).reshape(2 * rows, tokens)
    y_send = pick(mine, 1 - spot.y, 0).reshape(2 * rows, tokens)
    y_keep = pick(mine, spot.y, 0).reshape(2 * rows, tokens)
    return to_core, (x_send, x_keep), (y_send, y_keep)


def tie(now, after):
    out = lax.optimization_barrier((tuple(now), tuple(after)))
    return out[0]


class WeightSum:
    def __init__(self, spot, parts, x_first, rows):
        self.spot, self.x_first, self.rows = spot, x_first, rows
        self.to_core = parts[0]
        self.send_acts, self.keep_acts = parts[1] if x_first else parts[2]
        self.axis, self.here, self.bit = (1, spot.x, 2) if x_first else (0, spot.y, 4)
        self.here2, self.bit2 = (spot.y, 4) if x_first else (spot.x, 2)

    def core(self, grads):
        self.sent = bf16(dot_nn(self.to_core, grads))
        self.got = swap(self.sent, 1)
        return self.sent

    def first(self, got, grads):
        cols = grads.shape[1]
        got = got.reshape(2, 2, self.rows, cols)
        got_send = pick(got, 1 - self.here, self.axis).reshape(2 * self.rows, cols)
        got_keep = pick(got, self.here, self.axis).reshape(2 * self.rows, cols)
        self.sent = bf16(dot_nn(self.send_acts, grads) + f32(got_send))
        self.got = swap(self.sent, self.bit)
        self.kept = dot_nn(self.keep_acts, grads) + f32(got_keep)
        return self.kept

    def second(self, got, kept):
        cols = got.shape[1]
        got = got.reshape(2, self.rows, cols)
        kept = kept.reshape(2, self.rows, cols)
        self.sent = bf16(pick(kept, 1 - self.here2, 0) + f32(pick(got, 1 - self.here2, 0)))
        self.got = swap(self.sent, self.bit2)
        self.kept = pick(kept, self.here2, 0) + f32(pick(got, self.here2, 0))
        return self.sent

    def third(self, got, kept):
        self.sent = bf16(kept + f32(got))
        self.got = swap_rep(self.sent)
        return self.sent

    def result(self):
        return f32(self.sent) + f32(self.got)


def solution(mesh):
    batch_spec = P(('rep', 'shard'), None)
    row_spec = P(('rep', 'shard'))
    mat_spec = P('shard', None)
    vec_spec = P('shard')
    weight_specs = (mat_spec, vec_spec, mat_spec, vec_spec, mat_spec, vec_spec, mat_spec, mat_spec, mat_spec, mat_spec, vec_spec, vec_spec)
    in_specs = (batch_spec, row_spec, row_spec, batch_spec, P(None)) + weight_specs
    out_specs = (batch_spec,) + weight_specs

    def gather(part):
        return lax.all_gather(part, 'shard', axis=0, tiled=True)

    def per_device(x, seg_ids, positions, grad_y, num_tokens, w_q, b_q, w_k, b_k, w_v, b_v, w_o, w_gate, w_up, w_down, norm_attn, norm_mlp):
        tokens, width = x.shape
        ff = w_gate.shape[1]
        half = ff // 2
        q_cols, kv_cols = w_q.shape[1], w_k.shape[1]
        rows = w_q.shape[0]
        down_rows = w_down.shape[0]
        spot = Spot()
        inv_count = 1.0 / num_tokens[0].astype(jnp.float32)

        wqkv = gather(jnp.concatenate([w_q, w_k, w_v], axis=1))
        small_list = [b_q, b_k, b_v, norm_attn, norm_mlp]
        sizes = [v.shape[0] for v in small_list]
        small = lax.all_gather(stack_rows([f32(v)[None, :] for v in small_list]), 'shard', axis=0, tiled=False)
        wo = gather(w_o)
        wg0 = gather(w_gate[:, :half])
        wu0 = gather(w_up[:, :half])
        wdown = gather(w_down)
        wg1 = gather(w_gate[:, half:])
        wu1 = gather(w_up[:, half:])

        cuts = [small[:, i, :n].reshape(-1) for i, n in enumerate(sizes)]
        bias = jnp.concatenate(cuts[:3])
        gain_in, gain_mid = cuts[3], cuts[4]

        cos_t, sin_t = rope_tables(positions)
        start_row = jnp.broadcast_to((jnp.arange(tokens, dtype=jnp.int32) - positions)[None, :], (8, tokens))
        x_f = f32(x)
        inv_in = rms_inverse(x_f)
        normed_in = bf16(x_f * inv_in * gain_in)
        qkv_lin = dot_nn(normed_in, wqkv) + bias
        q_rot, k_rot, v_all, attn_out = attention_fwd(qkv_lin, cos_t, sin_t, start_row)
        resid = bf16(x_f + dot_nn(attn_out, wo))
        resid_f = f32(resid)
        inv_mid = rms_inverse(resid_f)
        normed_mid = bf16(resid_f * inv_mid * gain_mid)

        mid_parts = split_rows(spot, normed_mid, rows)
        o_parts = split_rows(spot, attn_out, rows)
        in_parts = split_rows(spot, normed_in, rows)
        flat_parts = jax.tree.leaves((mid_parts, o_parts, in_parts))

        def swiglu_back(gate_pre, up_proj, d_hid):
            sig_gate = jax.nn.sigmoid(gate_pre)
            act_gate = gate_pre * sig_gate
            d_gate = bf16(d_hid * up_proj * sig_gate * (1.0 + gate_pre * (1.0 - sig_gate)))
            return d_gate, bf16(d_hid * act_gate)

        def down_core(hidden):
            full = dot_tn(hidden, grad_y).reshape(2, 2, down_rows, width)
            return full, swap(bf16(pick(full, 1 - spot.core, 1)), 1)

        def down_x(full, got):
            mine = pick(full, spot.core, 1)
            sent = bf16(pick(mine, 1 - spot.x, 0) + f32(pick(got, 1 - spot.x, 0)))
            return sent, pick(mine, spot.x, 0) + f32(pick(got, spot.x, 0)), swap(sent, 2)

        n_mid, *flat_parts = tie([normed_mid] + flat_parts, [resid])
        mid_parts, o_parts, in_parts = jax.tree.unflatten(jax.tree.structure((mid_parts, o_parts, in_parts)), flat_parts)
        gate_sums = [WeightSum(spot, mid_parts, True, rows) for _ in range(2)]
        up_sums = [WeightSum(spot, mid_parts, False, rows) for _ in range(2)]

        gate0 = dot_nn(n_mid, wg0)
        up0 = dot_nn(n_mid, wu0)
        hidden0 = bf16(gate0 * jax.nn.sigmoid(gate0) * up0)
        hidden0, gate0, up0 = tie([hidden0, gate0, up0], [])
        full0, dgot0 = down_core(hidden0)
        d_hid0 = dot_nt(grad_y, tie([wdown], [full0])[0][:half])
        dg0, du0 = swiglu_back(gate0, up0, round_bf(d_hid0))

        dg0, du0, dgot0, full0 = tie([dg0, du0, dgot0, full0], [])
        dsent0, dkept0, dgot0x = down_x(full0, dgot0)
        c_g0 = gate_sums[0].core(dg0)
        c_u0 = up_sums[0].core(du0)
        dg0, du0, wg0b, wu0b = tie([dg0, du0, wg0, wu0], [c_g0, c_u0, dsent0, dkept0])
        d_mid = dot_nt(dg0, wg0b) + dot_nt(du0, wu0b)
        dg0, du0, got_g, got_u, n_mid = tie([dg0, du0, gate_sums[0].got, up_sums[0].got, n_mid], [d_mid])
        k_g0 = gate_sums[0].first(got_g, dg0)
        k_u0 = up_sums[0].first(got_u, du0)

        n_mid, wd1 = tie([n_mid, wdown], [k_g0, k_u0, gate_sums[0].sent, up_sums[0].sent])
        gate1 = dot_nn(n_mid, wg1)
        d_hid1 = bf16(dot_nt(grad_y, wd1[half:]))
        gate1, d_hid1 = tie([gate1, d_hid1], [])
        n_mid, = tie([n_mid], [gate1, d_hid1])
        up1 = dot_nn(n_mid, wu1)
        hidden1 = bf16(gate1 * jax.nn.sigmoid(gate1) * up1)
        dg1, du1 = swiglu_back(gate1, up1, f32(d_hid1))
        hidden1, dg1, du1, k_g0, k_u0, got_g, got_u = tie([hidden1, dg1, du1, k_g0, k_u0, gate_sums[0].got, up_sums[0].got], [])
        s_g0 = gate_sums[0].second(got_g, k_g0)
        s_u0 = up_sums[0].second(got_u, k_u0)
        c_g1 = gate_sums[1].core(dg1)
        c_u1 = up_sums[1].core(du1)
        hidden1, = tie([hidden1], [c_g1, c_u1, s_g0, s_u0])
        full1, dgot1 = down_core(hidden1)
        dg1, du1, got_g, got_u, full1 = tie([dg1, du1, gate_sums[1].got, up_sums[1].got, full1], [])
        k_g1 = gate_sums[1].first(got_g, dg1)
        k_u1 = up_sums[1].first(got_u, du1)
        dg1, du1, dgot1, full1, k_g1, k_u1, got_g, got_u = tie([dg1, du1, dgot1, full1, k_g1, k_u1, gate_sums[0].got, up_sums[0].got], [gate_sums[1].sent, up_sums[1].sent])
        t_g0 = gate_sums[0].third(got_g, gate_sums[0].kept)
        t_u0 = up_sums[0].third(got_u, up_sums[0].kept)
        dsent1, dkept1, dgot1x = down_x(full1, dgot1)
        dg1, du1, d_mid = tie([dg1, du1, d_mid], [t_g0, t_u0, dsent1, dkept1])
        d_mid = round_bf(d_mid + dot_nt(dg1, wg1) + dot_nt(du1, wu1))

        d_resid_norm, sum_norm_mlp = rms_back(d_mid, resid_f, inv_mid, gain_mid)
        d_resid = bf16(f32(grad_y) + d_resid_norm)
        d_resid, dkept0, dkept1, dgot0x, k_g1, k_u1, got_g, got_u = tie([d_resid, dkept0, dkept1, dgot0x, k_g1, k_u1, gate_sums[1].got, up_sums[1].got], [])
        s_g1 = gate_sums[1].second(got_g, k_g1)
        s_u1 = up_sums[1].second(got_u, k_u1)
        o_cut = width // 2
        o_sums = [WeightSum(spot, o_parts, first, rows) for first in (True, False)]
        c_o = [o_sums[i].core(d_resid[:, i * o_cut:(i + 1) * o_cut]) for i in range(2)]
        d_res_m, dgot1x = tie([d_resid, dgot1x], c_o + [s_g1, s_u1])
        low = spot.y == 0
        down_sent = bf16(jnp.where(low, dkept1 + f32(dgot1x), dkept0 + f32(dgot0x)))
        down_kept = jnp.where(low, dkept0 + f32(dgot0x), dkept1 + f32(dgot1x))
        down_got = swap(down_sent, 4)
        d_attn = bf16(dot_nt(d_res_m, wo))
        d_attn, got_g, got_u, got_o0, got_o1 = tie([d_attn, gate_sums[1].got, up_sums[1].got, o_sums[0].got, o_sums[1].got], [down_sent, down_kept])
        k_o = [o_sums[i].first(got, d_resid[:, i * o_cut:(i + 1) * o_cut]) for i, got in enumerate((got_o0, got_o1))]
        t_g1 = gate_sums[1].third(got_g, gate_sums[1].kept)
        t_u1 = up_sums[1].third(got_u, up_sums[1].kept)
        d_attn, = tie([d_attn], k_o + [t_g1, t_u1, o_sums[0].sent, o_sums[1].sent])
        d_q, d_k, d_v, sum_bq, sum_bk, sum_bv = attention_bwd(q_rot, k_rot, v_all, d_attn, cos_t, sin_t, start_row)
        d_qkv = jnp.concatenate([d_q, d_k, d_v], axis=1)
        d_qkv, k_o0, k_o1, got_o0, got_o1, down_got, down_kept = tie([d_qkv] + k_o + [o_sums[0].got, o_sums[1].got, down_got, down_kept], [])
        s_o = [o_sums[0].second(got_o0, k_o0), o_sums[1].second(got_o1, k_o1)]
        down_mine = bf16(down_kept + f32(down_got))
        down_rep = swap_rep(down_mine)
        q_cut = d_qkv.shape[1] // 2
        q_sums = [WeightSum(spot, in_parts, first, rows) for first in (True, False)]
        c_q = [q_sums[i].core(d_qkv[:, i * q_cut:(i + 1) * q_cut]) for i in range(2)]
        d_qkv, got_q0, got_q1 = tie([d_qkv, q_sums[0].got, q_sums[1].got], s_o + c_q + [down_mine])
        k_q = [q_sums[i].first(got, d_qkv[:, i * q_cut:(i + 1) * q_cut]) for i, got in enumerate((got_q0, got_q1))]
        d_qkv, got_o0, got_o1 = tie([d_qkv, o_sums[0].got, o_sums[1].got], k_q + [q_sums[0].sent, q_sums[1].sent])
        t_o = [o_sums[0].third(got_o0, o_sums[0].kept), o_sums[1].third(got_o1, o_sums[1].kept)]
        d_qkv, = tie([d_qkv], t_o)
        d_normed_in = round_bf(dot_nt(d_qkv, wqkv))
        d_x_norm, sum_norm_attn = rms_back(d_normed_in, x_f, inv_in, gain_in)
        grad_x = bf16(f32(d_resid) + d_x_norm)
        k_q0, k_q1, got_q0, got_q1, grad_x, sum_norm_attn = tie(k_q + [q_sums[0].got, q_sums[1].got, grad_x, sum_norm_attn], [])
        s_q = [q_sums[0].second(got_q0, k_q0), q_sums[1].second(got_q1, k_q1)]
        sum_norm_attn, = tie([sum_norm_attn], s_q)

        vecs = [sum_bq[0], sum_bk[0], sum_bv[0], sum_norm_attn, sum_norm_mlp]
        flat = stack_rows([v.reshape(8, 1, -1) for v in vecs])
        flat = pick(lax.psum(flat, ('rep', 'shard')), lax.axis_index('shard'), 0) * inv_count
        vec_out = [flat[i, :n] for i, n in enumerate(sizes)]
        for part in q_sums:
            part.third(part.got, part.kept)

        def joined(parts):
            return jnp.concatenate([part.result() for part in parts], axis=1) * inv_count

        qkv_sum = joined(q_sums)
        return (grad_x, qkv_sum[:, :q_cols], vec_out[0], qkv_sum[:, q_cols:q_cols + kv_cols], vec_out[1], qkv_sum[:, q_cols + kv_cols:], vec_out[2], joined(o_sums),
                joined(gate_sums), joined(up_sums), (f32(down_mine) + f32(down_rep)) * inv_count, vec_out[3], vec_out[4])

    return jax.shard_map(per_device, mesh=mesh, in_specs=in_specs, out_specs=out_specs, check_vma=False)
```

time: 3030 us -> 1380 us (0.46)
  waiting for transfers between devices: 1320 us -> 261 us
  matrix products: 1230 us -> 656 us
  Pallas kernels: 0 us -> 145 us
  local copies, waits for them, and re-layouts: 226 us -> 97 us
  blocking collectives: 77.2 us -> 11.3 us
  starting transfers between devices: 0.69 us -> 32.5 us
    reduce_scatter x7 -> x0, waiting for transfers between devices: 901 us -> none  [per_device(): lax.psum_scatter(full_grad, 'shard', scatter_dimension=0, tiled=True)]
    dot_general x50 -> x40, matrix products: 1090 us -> 656 us  [the longest x30 373 us: dot_nn(): lax.dot_general(a, b, (((1,), (0,)), ((), ())), preferred_element_type=jn...]
    psum x1, waiting for transfers between devices: 412 us -> 52.3 us  [per_device(): lax.psum(flat, ('rep', 'shard'))]
    pallas_call x0 -> x2, Pallas kernels: none -> 145 us  [the longest x1 81.6 us: attention_bwd(): pl.pallas_call(attn_bwd_kernel, grid=(HEADS,), in_specs=[head_spec(tokens...]
    sub x12 -> x0, matrix products: 144 us -> none  [block_probs(): return jax.nn.softmax(jnp.where(allowed, scores, -1e+30), axis=-1)]
    ppermute x0 -> x38, waiting for transfers between devices: none -> 112 us  [the longest x29 71.4 us: swap(): return lax.ppermute(arr, 'shard', [(s, s ^ bit) for s in range(8)])]
    all_gather x5 -> x7, waiting for transfers between devices: 0.05 us -> 94.1 us  [gather(): return lax.all_gather(part, 'shard', axis=0, tiled=True)]
    concatenate x7 -> x2, local copies, waits for them, and re-layouts: 61.6 us -> 0.1 us  [stack_rows(): rows = jnp.concatenate(rows, axis=-2)]
  transfers between devices with their start and end apart: 13 -> 46, of which waited for: 4 -> 10; matrix products, arithmetic and copies ran while one was open for 26% -> 64% of each run, Pallas kernels for 0% -> 11%
where the time goes in v1:
time: 1380 us; the launch traced here: 1370 us
  matrix products  656 us (48%)
  waiting for transfers between devices  261 us (19%)
  other arithmetic  152 us (11%)
  Pallas kernels  145 us (11%)
  local copies, waits for them, and re-layouts  97 us (7%)
  starting transfers between devices  32.5 us (2%)
  between operations  16.2 us (1%)
    dot_general x30, matrix products, dot_nn(): lax.dot_general(a, b, (((1,), (0,)), ((), ())), preferred_element_type=jn...  373 us
    dot_general x8, matrix products, dot_nt(): lax.dot_general(a, b, (((1,), (1,)), ((), ())), preferred_element_type=jn...  226 us
    all_gather x7, waiting for transfers between devices, gather(): return lax.all_gather(part, 'shard', axis=0, tiled=True)  94.1 us
    pallas_call x1, Pallas kernels, attention_bwd(): pl.pallas_call(attn_bwd_kernel, grid=(HEADS,), in_specs=[head_spec(tokens...  81.6 us
    ppermute x29, waiting for transfers between devices, swap(): return lax.ppermute(arr, 'shard', [(s, s ^ bit) for s in range(8)])  71.4 us
    convert_element_type x20, other arithmetic, bf16(): return arr.astype(jnp.bfloat16)  70.6 us
    pallas_call x1, Pallas kernels, attention_fwd(): pl.pallas_call(attn_fwd_kernel, grid=(HEADS,), in_specs=[head_spec(tokens...  63.1 us
    dot_general x2, matrix products, dot_tn(): lax.dot_general(a, b, (((0,), (0,)), ((), ())), preferred_element_type=jn...  56.2 us
  transfers between devices with their start and end apart: 46, of which 10 were waited for; matrix products, arithmetic and copies ran while one was open for 64% of the time, Pallas kernels for 11%

profile of v1, /device:TPU:0, one launch (start us, length us, event | category | flops | bytes accessed | tf_op | source)
XLA Modules:
  0.0 1370.3 jit_solution(3409448852962164304)
XLA Ops:
  58.1 16.3 %convolution_add_fusion.3.q_in.k_in.v_in = f32[1536,2048]{1,0:T(8,128)} fusion(bf16[1536,1536]{0,1:T(8,128)(2,1)} %fusion.25, bf16[1536,2048]{1,0:T(8,128)(2,1)} %all-gather.9.cloned.1.call-done, f32[2048]{0:T(1024)S(1)} %pad_maximum_fusion.4), kind=kOutput, calls=%fused_computation.65 | convolution fusion | flops 9666822144 | bytes 23601152 | tf_op jit(solution)/shard_map/dot_general | solution.py:29
  74.4 63.1 %attn_fwd.1 = (bf16[1536,1536]{1,0:T(8,128)(2,1)}, bf16[1536,256]{1,0:T(8,128)(2,1)S(1)}, bf16[1536,256]{1,0:T(8,128)(2,1)S(1)}, bf16[1536,1536]{1,0:T(8,128)(2,1)}) custom-call(f32[1536,2048]{1,0:T(8,128)} %convolution_add_fusion.3.q_in.k_in.v_in, f32[1536,2048]{1,0:T(8,128)} %convolution_add_fusion.3.q_in.k_in.v_in, ...), custom_call_target="tpu_custom_call" | custom-call | flops 34789236736 | bytes 30000000 | tf_op jit(solution)/shard_map/attn_fwd/pallas_call | solution.py:135
  171.4 32.8 %fusion.131 = f32[1536,4480]{1,0:T(8,128)} fusion(bf16[1536,1536]{0,1:T(8,128)(2,1)} %copy-done.6, bf16[1536,4480]{1,0:T(8,128)(2,1)} %all-gather.15.cloned.1.call-done), kind=kOutput, calls=%fused_computation.242 | convolution fusion | flops 21139292160 | bytes 46006272 | tf_op jit(solution)/shard_map/dot_general | solution.py:29
  204.2 37.9 %all-gather.17.cloned.1.call-done = bf16[1536,4480]{1,0:T(8,128)(2,1)} async-done(((bf16[192,4480]{1,0:T(8,128)(2,1)}), bf16[1536,4480]{1,0:T(8,128)(2,1)}) %all-gather.17.cloned.1.call-update) | async-done | bytes 13762576 | tf_op jit(solution)/shard_map/all_gather | solution.py:294
  242.1 39.9 %multiply_convert_fusion.1 = (bf16[1536,4480]{1,0:T(8,128)(2,1)}, f32[1536,4480]{1,0:T(8,128)}) fusion(f32[1536,4480]{1,0:T(8,128)} %fusion.131, bf16[1536,1536]{0,1:T(8,128)(2,1)} %copy-done.6, bf16[1536,4480]{1,0:T(8,128)(2,1)} %all-gather.17.cloned.1.call-done), kind=kOutput, calls=%fused_computation.16 | convolution fusion | flops 21180579840 | bytes 87293952 | tf_op jit(solution)/shard_map/dot_general | solution.py:29
  282.1 28.0 %fusion.132 = f32[4480,1536]{1,0:T(8,128)} fusion(bf16[1536,4480]{1,0:T(8,128)(2,1)} %get-tuple-element.128, bf16[1536,1536]{1,0:T(8,128)(2,1)} %param.19), kind=kOutput, calls=%fused_computation.243 | convolution fusion | flops 21139292160 | bytes 46006272 | tf_op jit(solution)/shard_map/dot_general | solution.py:37
  319.0 56.2 %all-gather.13.cloned.1.call-done = bf16[8960,1536]{1,0:T(8,128)(2,1)} async-done(((bf16[1120,1536]{1,0:T(8,128)(2,1)}), bf16[8960,1536]{1,0:T(8,128)(2,1)}) %all-gather.13.cloned.1.call-update) | async-done | bytes 27525136 | tf_op jit(solution)/shard_map/all_gather | solution.py:294
  375.3 49.7 %fusion.7 = (bf16[1536,4480]{1,0:T(8,128)(2,1)}, bf16[1536,4480]{1,0:T(8,128)(2,1)}) fusion(f32[1536,4480]{1,0:T(8,128)} %fusion.131, f32[1536,4480]{1,0:T(8,128)} %get-tuple-element.130, bf16[1536,1536]{1,0:T(8,128)(2,1)} %param.19, bf16[8960,1536]{1,0:T(8,128)(2,1)} %all-gather.13.cloned.1.call-done), kind=kOutput, calls=%fused_computation.11 | convolution fusion | flops 21235630080 | bytes 101056512 | tf_op jit(solution)/shard_map/dot_general | solution.py:33
  425.0 16.9 %convolution_convert_fusion.3 = bf16[768,4480]{1,0:T(8,128)(2,1)} fusion(bf16[768,1536]{1,0:T(8,128)(2,1)} %bitcast.315, bf16[1536,4480]{1,0:T(8,128)(2,1)} %get-tuple-element.146), kind=kOutput, calls=%fused_computation.63 | convolution fusion | flops 10573086720 | bytes 23003136 | tf_op jit(solution)/shard_map/dot_general | solution.py:29
  442.0 13.1 convolution_convert_fusion.4
  456.8 14.2 %convert_add_fusion.3 = (f32[1120,1536]{1,0:T(8,128)}, bf16[1120,1536]{1,0:T(8,128)(2,1)}) fusion(f32[2,2,1120,1536]{3,2,1,0:T(8,128)} %bitcast.283, s32[]{:T(128)S(6)} %select_n.161, s32[]{:T(128)S(6)} %select_n.159, bf16[2,1120,1536]{2,1,0:T(8,128)(2,1)} %collective-permute-done, s32[]{:T(128)S(6)} %select_n.160, s32[]{:T(128)S(6)} %select_n.156, ...), kind=kLoop, calls=%fused_computation.86 | loop fusion | flops 8601600 | bytes 30965780 | tf_op jit(solution)/shard_map/add | solution.py:351
  471.1 26.5 %fusion.133 = f32[1536,1536]{0,1:T(8,128)S(1)} fusion(bf16[1536,4480]{1,0:T(8,128)(2,1)} %get-tuple-element.143, bf16[1536,4480]{1,0:T(8,128)(2,1)} %all-gather.15.cloned.1.call-done), kind=kOutput, calls=%fused_computation.244 | convolution fusion | flops 21139292160 | bytes 36962304 | tf_op jit(solution)/shard_map/dot_general | solution.py:33
  497.6 31.1 %convolution_add_fusion.2 = f32[1536,1536]{0,1:T(8,128)} fusion(f32[1536,1536]{0,1:T(8,128)S(1)} %fusion.133, bf16[1536,4480]{1,0:T(8,128)(2,1)} %get-tuple-element.146, bf16[1536,4480]{1,0:T(8,128)(2,1)} %all-gather.17.cloned.1.call-done), kind=kOutput, calls=%fused_computation.37 | convolution fusion | flops 21141651456 | bytes 46399488 | tf_op jit(solution)/shard_map/dot_general | solution.py:33
  560.8 13.2 convolution_add_fusion.10
  573.9 13.1 convolution_add_fusion.11
  587.0 28.0 %fusion.9 = bf16[1536,4480]{1,0:T(8,128)(2,1)} fusion(bf16[1536,1536]{1,0:T(8,128)(2,1)S(1)} %bitcast.301, bf16[8960,1536]{1,0:T(8,128)(2,1)} %all-gather.13.cloned.1.call-done), kind=kOutput, calls=%fused_computation.29 | convolution fusion | flops 21146173440 | bytes 32243712 | tf_op jit(solution)/shard_map/dot_general | solution.py:33
  615.1 30.0 %fusion.134 = f32[1536,4480]{1,0:T(8,128)} fusion(bf16[1536,1536]{0,1:T(8,128)(2,1)} %copy-done.6, bf16[1536,4480]{1,0:T(8,128)(2,1)} %all-gather.19.cloned.1.call-done), kind=kOutput, calls=%fused_computation.245 | convolution fusion | flops 21139292160 | bytes 46006272 | tf_op jit(solution)/shard_map/dot_general | solution.py:29
  645.1 48.1 %fusion.2 = (bf16[1536,4480]{1,0:T(8,128)(2,1)}, bf16[1536,4480]{1,0:T(8,128)(2,1)}, bf16[1536,4480]{1,0:T(8,128)(2,1)}) fusion(bf16[1536,4480]{1,0:T(8,128)(2,1)} %fusion.9, f32[1536,4480]{1,0:T(8,128)} %fusion.134, bf16[1536,1536]{0,1:T(8,128)(2,1)} %copy-done.6, bf16[1536,4480]{1,0:T(8,128)(2,1)} %all-gather.21.cloned.1.call-done), kind=kOutput, calls=%fused_computation.4 | convolution fusion | flops 21249392640 | bytes 101056512 | tf_op jit(solution)/shard_map/dot_general | solution.py:29
  693.3 16.2 %convolution_convert_fusion.1 = bf16[768,4480]{1,0:T(8,128)(2,1)} fusion(bf16[768,1536]{1,0:T(8,128)(2,1)S(1)} %bitcast.317, bf16[1536,4480]{1,0:T(8,128)(2,1)} %get-tuple-element.176), kind=kOutput, calls=%fused_computation.61 | convolution fusion | flops 10573086720 | bytes 23003136 | tf_op jit(solution)/shard_map/dot_general | solution.py:29
  709.9 13.5 convolution_convert_fusion.2
  742.8 28.1 %fusion.135 = f32[4480,1536]{1,0:T(8,128)} fusion(bf16[1536,4480]{1,0:T(8,128)(2,1)} %get-tuple-element.162, bf16[1536,1536]{1,0:T(8,128)(2,1)} %param.19), kind=kOutput, calls=%fused_computation.246 | convolution fusion | flops 21139292160 | bytes 46006272 | tf_op jit(solution)/shard_map/dot_general | solution.py:37
  801.0 13.3 convolution_add_fusion.6
  826.8 12.8 convolution_add_fusion.7
  856.6 13.1 convert_add_fusion.1
  869.8 31.4 %convolution_add_fusion.1 = f32[1536,1536]{0,1:T(8,128)} fusion(f32[1536,1536]{0,1:T(8,128)} %convolution_add_fusion.2, bf16[1536,4480]{1,0:T(8,128)(2,1)} %get-tuple-element.175, bf16[1536,4480]{1,0:T(8,128)(2,1)} %all-gather.19.cloned.1.call-done), kind=kOutput, calls=%fused_computation.36 | convolution fusion | flops 21141651456 | bytes 46399488 | tf_op jit(solution)/shard_map/dot_general | solution.py:33
  901.2 32.8 %fusion.22 = (f32[1536]{0:T(1024)S(1)}, f32[1536]{0:T(1024)S(1)}, f32[1536,1536]{0,1:T(8,128)}) fusion(bf16[1536,1536]{0,1:T(8,128)(2,1)} %copy-done.9, f32[1536]{0:T(1024)S(1)} %copy-done.45, f32[1536]{0:T(1024)S(1)} %copy-done.49, f32[1536,1536]{0,1:T(8,128)} %convolution_add_fusion.1, bf16[1536,4480]{1,0:T(8,128)(2,1)} %get-tuple-element.176, ...), kind=kOutput, calls=%fused_computation.47 | convolution fusion | flops 21160521728 | bytes 51142656 | tf_op jit(solution)/shard_map/dot_general | solution.py:33
  969.2 51.8 %collective-permute-done.13 = bf16[1120,1536]{1,0:T(8,128)(2,1)S(1)} collective-permute-done((bf16[1120,1536]{1,0:T(8,128)(2,1)}, bf16[1120,1536]{1,0:T(8,128)(2,1)S(1)}, u32[]{:S(2)}, u32[]{:S(2)}) %collective-permute-start.13) | collective-permute-done | bytes 3440672 | tf_op jit(solution)/shard_map/ppermute | solution.py:197
  1041.1 14.4 %collective-permute-done.15 = bf16[192,4480]{1,0:T(8,128)(2,1)S(1)} collective-permute-done((bf16[192,4480]{1,0:T(8,128)(2,1)}, bf16[192,4480]{1,0:T(8,128)(2,1)S(1)}, u32[]{:S(2)}, u32[]{:S(2)}) %collective-permute-start.15) | collective-permute-done | bytes 1720352 | tf_op jit(solution)/shard_map/ppermute | solution.py:197
  1078.9 81.6 %attn_bwd.1 = (bf16[1536,1536]{1,0:T(8,128)(2,1)}, bf16[1536,256]{1,0:T(8,128)(2,1)S(1)}, bf16[1536,256]{1,0:T(8,128)(2,1)S(1)}, f32[8,1536]{1,0:T(8,128)S(1)}, ...) custom-call(bf16[1536,1536]{1,0:T(8,128)(2,1)} %get-tuple-element.124.q_ref, bf16[1536,256]{1,0:T(8,128)(2,1)S(1)} %get-tuple-element.125.k_ref, ...), custom_call_target="tpu_custom_call" | custom-call | flops 65229815808 | bytes 30000000 | tf_op jit(solution)/shard_map/attn_bwd/pallas_call | solution.py:162
  1216.9 15.0 %fusion.33 = (f32[1536]{0:T(1024)S(1)}, f32[1536]{0:T(1024)S(1)}, f32[1536,1536]{0,1:T(8,128)S(1)}) fusion(bf16[1536,1536]{0,1:T(8,128)(2,1)S(1)} %bitcast.256, f32[1536]{0:T(1024)S(1)} %copy-done.43, f32[1536]{0:T(1024)S(1)} %copy-done.47, bf16[1536,2048]{1,0:T(8,128)(2,1)} %copy-done.13, bf16[1536,2048]{1,0:T(8,128)(2,1)} %all-gather.9.cloned.1.call-done), kind=kOutput, calls=%fused_computation.58 | convolution fusion | flops 9682546688 | bytes 26763264 | tf_op jit(solution)/shard_map/dot_general | solution.py:33
  1237.0 24.6 %collective-permute-done.31 = bf16[192,768]{1,0:T(8,128)(2,1)} collective-permute-done((bf16[192,768]{1,0:T(8,128)(2,1)}, bf16[192,768]{1,0:T(8,128)(2,1)}, u32[]{:S(2)}, u32[]{:S(2)}) %collective-permute-start.31) | collective-permute-done | bytes 294944 | tf_op jit(solution)/shard_map/ppermute | solution.py:201
  1280.5 52.3 %all-reduce.14.cloned.1.call-done = f32[8,8,256]{2,1,0:T(8,128)} async-done(((f32[8,8,256]{2,1,0:T(8,128)}), f32[8,8,256]{2,1,0:T(8,128)}) %all-reduce.14.cloned.1.call-update) | async-done | bytes 65552 | tf_op jit(solution)/shard_map/psum | solution.py:443
  (409 shorter events, 394.7 us)
Async XLA Ops:
  9.4 128.7 %all-gather.11.cloned.1.call-start = ((), (), s32[]{:S(2)}) async-start(), calls=%async_computation.1 | async-start | bytes 5308416 | tf_op jit(solution)/shard_map/all_gather | solution.py:294
  10.2 161.3 %all-gather.15.cloned.1.call-start = ((), (), s32[]{:S(2)}) async-start(), calls=%async_computation.3 | async-start | bytes 15482880 | tf_op jit(solution)/shard_map/all_gather | solution.py:294
  14.5 227.6 %all-gather.17.cloned.1.call-start = ((), (), s32[]{:S(2)}) async-start(), calls=%async_computation.4 | async-start | bytes 15482880 | tf_op jit(solution)/shard_map/all_gather | solution.py:294
  16.7 358.6 %all-gather.13.cloned.1.call-start = ((), (), s32[]{:S(2)}) async-start(), calls=%async_computation.2 | async-start | bytes 30965760 | tf_op jit(solution)/shard_map/all_gather | solution.py:294
  17.3 597.8 %all-gather.19.cloned.1.call-start = ((), (), s32[]{:S(2)}) async-start(), calls=%async_computation.5 | async-start | bytes 15482880 | tf_op jit(solution)/shard_map/all_gather | solution.py:294
  17.8 627.3 %all-gather.21.cloned.1.call-start = ((), (), s32[]{:S(2)}) async-start(), calls=%async_computation.6 | async-start | bytes 15482880 | tf_op jit(solution)/shard_map/all_gather | solution.py:294
  18.6 1314.3 %all-reduce.14.cloned.1.call-start = ((), (), s32[]{:S(2)}) async-start(), calls=%async_computation.7 | async-start | bytes 131072 | tf_op jit(solution)/shard_map/psum | solution.py:443
  318.8 106.2 %collective-permute-start = (bf16[2,1120,1536]{2,1,0:T(8,128)(2,1)}, bf16[2,1120,1536]{2,1,0:T(8,128)(2,1)}, u32[]{:S(2)}, u32[]{:S(2)}) collective-permute-start(bf16[2,1120,1536]{2,1,0:T(8,128)(2,1)} %fusion.39), channel_id=1, source_target_pairs={{0,1},{1,0},{2,3},{3,2},{4,5},{5,4},{6,7},{7,6},{8,9},{9,8},{10,11... | collective-permute-start | bytes 20643848 | tf_op jit(solution)/shard_map/ppermute | solution.py:197
  455.1 73.6 %collective-permute-start.2 = (bf16[768,4480]{1,0:T(8,128)(2,1)}, bf16[768,4480]{1,0:T(8,128)(2,1)}, u32[]{:S(2)}, u32[]{:S(2)}) collective-permute-start(bf16[768,4480]{1,0:T(8,128)(2,1)} %convolution_convert_fusion.3), channel_id=1, source_target_pairs={{0,1},{1,0},{2,3},{3,2},{4,5},{5,4},{6,7},{7,6},{8,9},{9,8},{10,11... | collective-permute-start | bytes 20643848 | tf_op jit(solution)/shard_map/ppermute | solution.py:197
  456.8 71.9 %collective-permute-start.1 = (bf16[768,4480]{1,0:T(8,128)(2,1)}, bf16[768,4480]{1,0:T(8,128)(2,1)}, u32[]{:S(2)}, u32[]{:S(2)}) collective-permute-start(bf16[768,4480]{1,0:T(8,128)(2,1)} %convolution_convert_fusion.4), channel_id=1, source_target_pairs={{0,1},{1,0},{2,3},{3,2},{4,5},{5,4},{6,7},{7,6},{8,9},{9,8},{10,11... | collective-permute-start | bytes 20643848 | tf_op jit(solution)/shard_map/ppermute | solution.py:197
  544.7 148.6 %collective-permute-start.4 = (bf16[384,4480]{1,0:T(8,128)(2,1)}, bf16[384,4480]{1,0:T(8,128)(2,1)}, u32[]{:S(2)}, u32[]{:S(2)}) collective-permute-start(bf16[384,4480]{1,0:T(8,128)(2,1)} %fusion.36), channel_id=1, source_target_pairs={{0,4},{1,5},{2,6},{3,7},{4,0},{5,1},{6,2},{7,3},{8,12},{9,13},{10,... | collective-permute-start | bytes 10321928 | tf_op jit(solution)/shard_map/ppermute | solution.py:197
  560.7 132.5 %collective-permute-start.3 = (bf16[384,4480]{1,0:T(8,128)(2,1)}, bf16[384,4480]{1,0:T(8,128)(2,1)}, u32[]{:S(2)}, u32[]{:S(2)}) collective-permute-start(bf16[384,4480]{1,0:T(8,128)(2,1)} %fusion.35), channel_id=1, source_target_pairs={{0,2},{1,3},{2,0},{3,1},{4,6},{5,7},{6,4},{7,5},{8,10},{9,11},{10,... | collective-permute-start | bytes 10321928 | tf_op jit(solution)/shard_map/ppermute | solution.py:197
  709.5 70.2 %collective-permute-start.6 = (bf16[768,4480]{1,0:T(8,128)(2,1)}, bf16[768,4480]{1,0:T(8,128)(2,1)}, u32[]{:S(2)}, u32[]{:S(2)}) collective-permute-start(bf16[768,4480]{1,0:T(8,128)(2,1)} %convolution_convert_fusion.1), channel_id=1, source_target_pairs={{0,1},{1,0},{2,3},{3,2},{4,5},{5,4},{6,7},{7,6},{8,9},{9,8},{10,11... | collective-permute-start | bytes 20643848 | tf_op jit(solution)/shard_map/ppermute | solution.py:197
  730.8 221.1 %collective-permute-start.10 = (bf16[1120,1536]{1,0:T(8,128)(2,1)}, bf16[1120,1536]{1,0:T(8,128)(2,1)}, u32[]{:S(2)}, u32[]{:S(2)}) collective-permute-start(bf16[1120,1536]{1,0:T(8,128)(2,1)} %get-tuple-element.274), channel_id=1, source_target_pairs={{0,2},{1,3},{2,0},{3,1},{4,6},{5,7},{6,4},{7,5},{8,10},{9,11},{10,... | collective-permute-start | bytes 10321928 | tf_op jit(solution)/shard_map/ppermute | solution.py:197
  736.8 107.9 %collective-permute-start.9 = (bf16[192,4480]{1,0:T(8,128)(2,1)}, bf16[192,4480]{1,0:T(8,128)(2,1)S(1)}, u32[]{:S(2)}, u32[]{:S(2)}) collective-permute-start(bf16[192,4480]{1,0:T(8,128)(2,1)} %fusion.73), channel_id=1, source_target_pairs={{0,2},{1,3},{2,0},{3,1},{4,6},{5,7},{6,4},{7,5},{8,10},{9,11},{10,... | collective-permute-start | bytes 5160968 | tf_op jit(solution)/shard_map/ppermute | solution.py:197
  740.8 105.6 %collective-permute-start.8 = (bf16[192,4480]{1,0:T(8,128)(2,1)}, bf16[192,4480]{1,0:T(8,128)(2,1)}, u32[]{:S(2)}, u32[]{:S(2)}) collective-permute-start(bf16[192,4480]{1,0:T(8,128)(2,1)} %fusion.72), channel_id=1, source_target_pairs={{0,4},{1,5},{2,6},{3,7},{4,0},{5,1},{6,2},{7,3},{8,12},{9,13},{10,... | collective-permute-start | bytes 5160968 | tf_op jit(solution)/shard_map/ppermute | solution.py:197
  779.6 66.8 %collective-permute-start.7 = (bf16[2,1120,1536]{2,1,0:T(8,128)(2,1)}, bf16[2,1120,1536]{2,1,0:T(8,128)(2,1)S(1)}, u32[]{:S(2)}, u32[]{:S(2)}) collective-permute-start(bf16[2,1120,1536]{2,1,0:T(8,128)(2,1)} %fusion.40), channel_id=1, source_target_pairs={{0,1},{1,0},{2,3},{3,2},{4,5},{5,4},{6,7},{7,6},{8,9},{9,8},{10,11... | collective-permute-start | bytes 20643848 | tf_op jit(solution)/shard_map/ppermute | solution.py:197
  800.9 151.0 %collective-permute-start.12 = (bf16[384,4480]{1,0:T(8,128)(2,1)}, bf16[384,4480]{1,0:T(8,128)(2,1)}, u32[]{:S(2)}, u32[]{:S(2)}) collective-permute-start(bf16[384,4480]{1,0:T(8,128)(2,1)} %fusion.38), channel_id=1, source_target_pairs={{0,4},{1,5},{2,6},{3,7},{4,0},{5,1},{6,2},{7,3},{8,12},{9,13},{10,... | collective-permute-start | bytes 10321928 | tf_op jit(solution)/shard_map/ppermute | solution.py:197
  844.7 107.2 %collective-permute-start.11 = (bf16[384,4480]{1,0:T(8,128)(2,1)}, bf16[384,4480]{1,0:T(8,128)(2,1)}, u32[]{:S(2)}, u32[]{:S(2)}) collective-permute-start(bf16[384,4480]{1,0:T(8,128)(2,1)} %fusion.37), channel_id=1, source_target_pairs={{0,2},{1,3},{2,0},{3,1},{4,6},{5,7},{6,4},{7,5},{8,10},{9,11},{10,... | collective-permute-start | bytes 10321928 | tf_op jit(solution)/shard_map/ppermute | solution.py:197
  854.5 89.0 %collective-permute-start.35 = (bf16[192,4480]{1,0:T(8,128)(2,1)}, bf16[192,4480]{1,0:T(8,128)(2,1)}, u32[]{:S(2)}, u32[]{:S(2)}) collective-permute-start(bf16[192,4480]{1,0:T(8,128)(2,1)} %fusion.46), channel_id=1, source_target_pairs={{0,8},{8,0},{1,9},{9,1},{2,10},{10,2},{3,11},{11,3},{4,12},{12,4},... | collective-permute-start | bytes 5160968 | tf_op jit(solution)/shard_map/ppermute | solution.py:201
  854.6 93.5 %collective-permute-start.33 = (bf16[192,4480]{1,0:T(8,128)(2,1)S(1)}, bf16[192,4480]{1,0:T(8,128)(2,1)}, u32[]{:S(2)}, u32[]{:S(2)}) collective-permute-start(bf16[192,4480]{1,0:T(8,128)(2,1)S(1)} %fusion.47), channel_id=1, source_target_pairs={{0,8},{8,0},{1,9},{9,1},{2,10},{10,2},{3,11},{11,3},{4,12},{12,4},... | collective-permute-start | bytes 5160968 | tf_op jit(solution)/shard_map/ppermute | solution.py:201
  943.5 77.5 %collective-permute-start.13 = (bf16[1120,1536]{1,0:T(8,128)(2,1)}, bf16[1120,1536]{1,0:T(8,128)(2,1)S(1)}, u32[]{:S(2)}, u32[]{:S(2)}) collective-permute-start(bf16[1120,1536]{1,0:T(8,128)(2,1)} %get-tuple-element.272), channel_id=1, source_target_pairs={{0,2},{1,3},{2,0},{3,1},{4,6},{5,7},{6,4},{7,5},{8,10},{9,11},{10,... | collective-permute-start | bytes 10321928 | tf_op jit(solution)/shard_map/ppermute | solution.py:197
  955.9 99.6 %collective-permute-start.15 = (bf16[192,4480]{1,0:T(8,128)(2,1)}, bf16[192,4480]{1,0:T(8,128)(2,1)S(1)}, u32[]{:S(2)}, u32[]{:S(2)}) collective-permute-start(bf16[192,4480]{1,0:T(8,128)(2,1)} %fusion.75), channel_id=1, source_target_pairs={{0,2},{1,3},{2,0},{3,1},{4,6},{5,7},{6,4},{7,5},{8,10},{9,11},{10,... | collective-permute-start | bytes 5160968 | tf_op jit(solution)/shard_map/ppermute | solution.py:197
  960.6 94.9 %collective-permute-start.14 = (bf16[192,4480]{1,0:T(8,128)(2,1)}, bf16[192,4480]{1,0:T(8,128)(2,1)}, u32[]{:S(2)}, u32[]{:S(2)}) collective-permute-start(bf16[192,4480]{1,0:T(8,128)(2,1)} %fusion.74), channel_id=1, source_target_pairs={{0,4},{1,5},{2,6},{3,7},{4,0},{5,1},{6,2},{7,3},{8,12},{9,13},{10,... | collective-permute-start | bytes 5160968 | tf_op jit(solution)/shard_map/ppermute | solution.py:197
  965.6 75.4 %collective-permute-start.17 = (bf16[768,768]{1,0:T(8,128)(2,1)}, bf16[768,768]{1,0:T(8,128)(2,1)}, u32[]{:S(2)}, u32[]{:S(2)}) collective-permute-start(bf16[768,768]{1,0:T(8,128)(2,1)} %fusion.87), channel_id=1, source_target_pairs={{0,1},{1,0},{2,3},{3,2},{4,5},{5,4},{6,7},{7,6},{8,9},{9,8},{10,11... | collective-permute-start | bytes 3538952 | tf_op jit(solution)/shard_map/ppermute | solution.py:197
  968.7 72.4 %collective-permute-start.16 = (bf16[768,768]{1,0:T(8,128)(2,1)}, bf16[768,768]{1,0:T(8,128)(2,1)}, u32[]{:S(2)}, u32[]{:S(2)}) collective-permute-start(bf16[768,768]{1,0:T(8,128)(2,1)} %fusion.84), channel_id=1, source_target_pairs={{0,1},{1,0},{2,3},{3,2},{4,5},{5,4},{6,7},{7,6},{8,9},{9,8},{10,11... | collective-permute-start | bytes 3538952 | tf_op jit(solution)/shard_map/ppermute | solution.py:197
  1027.5 137.7 %collective-permute-start.20 = (bf16[1120,1536]{1,0:T(8,128)(2,1)}, bf16[1120,1536]{1,0:T(8,128)(2,1)}, u32[]{:S(2)}, u32[]{:S(2)}) collective-permute-start(bf16[1120,1536]{1,0:T(8,128)(2,1)} %get-tuple-element.276), channel_id=1, source_target_pairs={{0,4},{1,5},{2,6},{3,7},{4,0},{5,1},{6,2},{7,3},{8,12},{9,13},{10,... | collective-permute-start | bytes 10321928 | tf_op jit(solution)/shard_map/ppermute | solution.py:197
  1068.4 96.8 %collective-permute-start.19 = (bf16[384,768]{1,0:T(8,128)(2,1)}, bf16[384,768]{1,0:T(8,128)(2,1)}, u32[]{:S(2)}, u32[]{:S(2)}) collective-permute-start(bf16[384,768]{1,0:T(8,128)(2,1)} %fusion.110), channel_id=1, source_target_pairs={{0,4},{1,5},{2,6},{3,7},{4,0},{5,1},{6,2},{7,3},{8,12},{9,13},{10,... | collective-permute-start | bytes 1769480 | tf_op jit(solution)/shard_map/ppermute | solution.py:197
  1072.0 93.2 %collective-permute-start.18 = (bf16[384,768]{1,0:T(8,128)(2,1)}, bf16[384,768]{1,0:T(8,128)(2,1)}, u32[]{:S(2)}, u32[]{:S(2)}) collective-permute-start(bf16[384,768]{1,0:T(8,128)(2,1)} %fusion.113), channel_id=1, source_target_pairs={{0,2},{1,3},{2,0},{3,1},{4,6},{5,7},{6,4},{7,5},{8,10},{9,11},{10,... | collective-permute-start | bytes 1769480 | tf_op jit(solution)/shard_map/ppermute | solution.py:197
  1072.5 111.1 %collective-permute-start.36 = (bf16[192,4480]{1,0:T(8,128)(2,1)}, bf16[192,4480]{1,0:T(8,128)(2,1)}, u32[]{:S(2)}, u32[]{:S(2)}) collective-permute-start(bf16[192,4480]{1,0:T(8,128)(2,1)} %fusion.44), channel_id=1, source_target_pairs={{0,8},{8,0},{1,9},{9,1},{2,10},{10,2},{3,11},{11,3},{4,12},{12,4},... | collective-permute-start | bytes 5160968 | tf_op jit(solution)/shard_map/ppermute | solution.py:201
  1073.2 113.8 %collective-permute-start.34 = (bf16[192,4480]{1,0:T(8,128)(2,1)}, bf16[192,4480]{1,0:T(8,128)(2,1)}, u32[]{:S(2)}, u32[]{:S(2)}) collective-permute-start(bf16[192,4480]{1,0:T(8,128)(2,1)} %fusion.45), channel_id=1, source_target_pairs={{0,8},{8,0},{1,9},{9,1},{2,10},{10,2},{3,11},{11,3},{4,12},{12,4},... | collective-permute-start | bytes 5160968 | tf_op jit(solution)/shard_map/ppermute | solution.py:201
  1178.9 178.4 %collective-permute-start.37 = (bf16[1120,1536]{1,0:T(8,128)(2,1)S(1)}, bf16[1120,1536]{1,0:T(8,128)(2,1)}, u32[]{:S(2)}, u32[]{:S(2)}) collective-permute-start(bf16[1120,1536]{1,0:T(8,128)(2,1)S(1)} %add_convert_fusion), channel_id=1, source_target_pairs={{0,8},{8,0},{1,9},{9,1},{2,10},{10,2},{3,11},{11,3},{4,12},{12,4},... | collective-permute-start | bytes 10321928 | tf_op jit(solution)/shard_map/ppermute | solution.py:201
  (101 other events, 2033.2 us)
Sparse Core Ops, SparseCore 0:
  10.4 44.6 all-gather.8
  57.0 35.0 all-gather.10
  93.9 73.2 all-gather.14
  168.9 73.2 all-gather.16
  243.8 131.4 all-gather.12
  377.0 73.2 all-gather.18
  452.1 73.2 all-gather.20
  1270.5 62.3 all-reduce.13

commit v2 on v1

--- a/solution.py
+++ b/solution.py
@@ -14,6 +14,7 @@
 EPS = 1e-6
 QB = 256
 SCALE = HEAD_DIM ** -0.5
+LOG2E = 1.4426950408889634
 
 
 def rope_tables(positions):
@@ -41,11 +42,17 @@
     return lax.reduce_precision(vals, 8, 7)
 
 
-def masked_scores(k_part, q_blk, first_row, start_row):
-    s_t = dot_nt(k_part, q_blk) * SCALE
-    key_idx = lax.broadcasted_iota(jnp.int32, s_t.shape, 0)
-    row_idx = lax.broadcasted_iota(jnp.int32, s_t.shape, 1) + first_row
-    return jnp.where((key_idx >= start_row) & (key_idx <= row_idx), s_t, -1e30)
+def exp_scores(k_part, q_blk, first_row, start_row):
+    s_t = dot_nt(k_part, q_blk)
+    key_idx = lax.broadcasted_iota(jnp.int32, (QB, QB), 0)
+    row_idx = lax.broadcasted_iota(jnp.int32, (QB, QB), 1)
+    parts = []
+    for base in range(0, first_row, QB):
+        parts.append(jnp.where(key_idx >= start_row - base, s_t[base:base + QB], -1e30))
+    parts.append(jnp.where((key_idx >= start_row - first_row) & (key_idx <= row_idx), s_t[first_row:], -1e30))
+    s_t = jnp.concatenate(parts, axis=0)
+    e_t = jnp.exp2((s_t - jnp.max(s_t, axis=0, keepdims=True)) * (SCALE * LOG2E))
+    return e_t, 1.0 / jnp.sum(e_t, axis=0, keepdims=True)
 
 
 def attn_fwd_kernel(q_in, k_in, v_in, cos_ref, sin_ref, start_ref, q_out, k_out, v_out, o_out, vt_scr):
@@ -63,9 +70,8 @@
     q_out[...] = (q_f * cos_ref[...] + pltpu.roll(q_f, HEAD_DIM // 2, 1) * sin_ref[...]).astype(jnp.bfloat16)
     for first in range(0, tokens, QB):
         keys = first + QB
-        s_t = masked_scores(k_out[:keys, :], q_out[first:keys, :], first, start_ref[0:1, first:keys])
-        e_t = jnp.exp(s_t - jnp.max(s_t, axis=0, keepdims=True))
-        p_t = (e_t / jnp.sum(e_t, axis=0, keepdims=True)).astype(jnp.bfloat16)
+        e_t, inv_sum = exp_scores(k_out[:keys, :], q_out[first:keys, :], first, start_ref[0:1, first:keys])
+        p_t = (e_t * inv_sum).astype(jnp.bfloat16)
         o_t = dot_nn(vt_scr[:, :keys], p_t)
         o_out[first:keys, :] = o_t.T.astype(jnp.bfloat16)
 
@@ -88,9 +94,8 @@
         keys = first + QB
         q_blk = q_ref[first:keys, :]
         do_blk = do_ref[first:keys, :]
-        s_t = masked_scores(k_ref[:keys, :], q_blk, first, start_ref[0:1, first:keys])
-        e_t = jnp.exp(s_t - jnp.max(s_t, axis=0, keepdims=True))
-        p_t = e_t / jnp.sum(e_t, axis=0, keepdims=True)
+        e_t, inv_sum = exp_scores(k_ref[:keys, :], q_blk, first, start_ref[0:1, first:keys])
+        p_t = e_t * inv_sum
         dp_t = dot_nt(v_ref[:keys, :], do_blk)
         dv_acc[:keys, :] += dot_nn(p_t.astype(jnp.bfloat16), do_blk)
         delta = jnp.sum(p_t * dp_t, axis=0, keepdims=True)
@@ -150,31 +155,31 @@
     )(qkv_lin, qkv_lin, qkv_lin, cos_t, sin_t, start_row)
 
 
-def attention_bwd(q_rot, k_rot, v_all, d_out, cos_t, sin_t, start_row):
+def attention_bwd(kv_head, q_rot, k_rot, v_all, d_out, cos_t, sin_t, start_row):
     tokens = q_rot.shape[0]
     table = whole_spec((tokens, HEAD_DIM))
-    pairs = HEADS * tokens * tokens * 0.6
+    pairs = GROUP * tokens * tokens * 0.6
+    q_in = head_spec(tokens, kv_head * GROUP)
+    kv_in = pl.BlockSpec((tokens, HEAD_DIM), lambda h: (0, kv_head))
     row_q = pl.BlockSpec((8, HEAD_DIM), lambda h: (0, h))
-    row_kv = pl.BlockSpec((8, HEAD_DIM), lambda h: (0, h // GROUP))
     acc = pltpu.VMEM((tokens, HEAD_DIM), jnp.float32)
-    q_cols = HEADS * HEAD_DIM
-    kv_cols = KV_HEADS * HEAD_DIM
+    q_cols = GROUP * HEAD_DIM
     return pl.pallas_call(
         attn_bwd_kernel,
-        grid=(HEADS,),
-        in_specs=[head_spec(tokens, 0), kv_spec(tokens, 0), kv_spec(tokens, 0), head_spec(tokens, 0), table, table, whole_spec((8, tokens))],
-        out_specs=[head_spec(tokens, 0), kv_spec(tokens, 0), kv_spec(tokens, 0), row_q, row_kv, row_kv],
+        grid=(GROUP,),
+        in_specs=[q_in, kv_in, kv_in, q_in, table, table, whole_spec((8, tokens))],
+        out_specs=[head_spec(tokens, 0), table, table, row_q, whole_spec((8, HEAD_DIM)), whole_spec((8, HEAD_DIM))],
         out_shape=[
             jax.ShapeDtypeStruct((tokens, q_cols), jnp.bfloat16),
-            jax.ShapeDtypeStruct((tokens, kv_cols), jnp.bfloat16),
-            jax.ShapeDtypeStruct((tokens, kv_cols), jnp.bfloat16),
+            jax.ShapeDtypeStruct((tokens, HEAD_DIM), jnp.bfloat16),
+            jax.ShapeDtypeStruct((tokens, HEAD_DIM), jnp.bfloat16),
             jax.ShapeDtypeStruct((8, q_cols), jnp.float32),
-            jax.ShapeDtypeStruct((8, kv_cols), jnp.float32),
-            jax.ShapeDtypeStruct((8, kv_cols), jnp.float32),
+            jax.ShapeDtypeStruct((8, HEAD_DIM), jnp.float32),
+            jax.ShapeDtypeStruct((8, HEAD_DIM), jnp.float32),
         ],
         scratch_shapes=[acc, acc, pltpu.VMEM((HEAD_DIM, tokens), jnp.bfloat16), acc],
         compiler_params=pltpu.CompilerParams(dimension_semantics=("arbitrary",), vmem_limit_bytes=48 * 1024 * 1024),
-        cost_estimate=pl.CostEstimate(flops=int(pairs * 128 * 30), bytes_accessed=30000000, transcendentals=int(pairs)),
+        cost_estimate=pl.CostEstimate(flops=int(pairs * 128 * 30), bytes_accessed=15000000, transcendentals=int(pairs)),
         name="attn_bwd",
     )(q_rot, k_rot, v_all, d_out, cos_t, sin_t, start_row)
 
@@ -226,13 +231,14 @@
 def split_rows(spot, acts, rows):
     tokens = acts.shape[0]
     cut = acts.T.reshape(2, 2, 2, rows, tokens)
-    to_core = pick(cut, 1 - spot.core, 2).reshape(4 * rows, tokens)
-    mine = pick(cut, spot.core, 2)
-    x_send = pick(mine, 1 - spot.x, 1).reshape(2 * rows, tokens)
-    x_keep = pick(mine, spot.x, 1).reshape(2 * rows, tokens)
-    y_send = pick(mine, 1 - spot.y, 0).reshape(2 * rows, tokens)
-    y_keep = pick(mine, spot.y, 0).reshape(2 * rows, tokens)
-    return to_core, (x_send, x_keep), (y_send, y_keep)
+    out = []
+    for axis, here in ((1, spot.x), (0, spot.y)):
+        pair = []
+        for core in (1 - spot.core, spot.core):
+            mine = pick(cut, core, 2)
+            pair.append(jnp.stack([pick(mine, 1 - here, axis), pick(mine, here, axis)]).reshape(4 * rows, tokens))
+        out.append(tuple(pair))
+    return tuple(out)
 
 
 def tie(now, after):
@@ -243,9 +249,8 @@
 class WeightSum:
     def __init__(self, spot, parts, x_first, rows):
         self.spot, self.x_first, self.rows = spot, x_first, rows
-        self.to_core = parts[0]
-        self.send_acts, self.keep_acts = parts[1] if x_first else parts[2]
-        self.axis, self.here, self.bit = (1, spot.x, 2) if x_first else (0, spot.y, 4)
+        self.to_core, self.own_acts = parts[0] if x_first else parts[1]
+        self.bit = 2 if x_first else 4
         self.here2, self.bit2 = (spot.y, 4) if x_first else (spot.x, 2)
 
     def core(self, grads):
@@ -254,13 +259,10 @@
         return self.sent
 
     def first(self, got, grads):
-        cols = grads.shape[1]
-        got = got.reshape(2, 2, self.rows, cols)
-        got_send = pick(got, 1 - self.here, self.axis).reshape(2 * self.rows, cols)
-        got_keep = pick(got, self.here, self.axis).reshape(2 * self.rows, cols)
-        self.sent = bf16(dot_nn(self.send_acts, grads) + f32(got_send))
+        own, = tie([dot_nn(self.own_acts, grads) + f32(got)], [])
+        self.sent = bf16(own[:2 * self.rows])
         self.got = swap(self.sent, self.bit)
-        self.kept = dot_nn(self.keep_acts, grads) + f32(got_keep)
+        self.kept = own[2 * self.rows:]
         return self.kept
 
     def second(self, got, kept):
@@ -384,66 +386,80 @@
         hidden1, dg1, du1, k_g0, k_u0, got_g, got_u = tie([hidden1, dg1, du1, k_g0, k_u0, gate_sums[0].got, up_sums[0].got], [])
         s_g0 = gate_sums[0].second(got_g, k_g0)
         s_u0 = up_sums[0].second(got_u, k_u0)
+        hidden1, = tie([hidden1], [s_g0, s_u0])
+        full1, dgot1 = down_core(hidden1)
+        dg1, du1, full1 = tie([dg1, du1, full1], [])
         c_g1 = gate_sums[1].core(dg1)
         c_u1 = up_sums[1].core(du1)
-        hidden1, = tie([hidden1], [c_g1, c_u1, s_g0, s_u0])
-        full1, dgot1 = down_core(hidden1)
-        dg1, du1, got_g, got_u, full1 = tie([dg1, du1, gate_sums[1].got, up_sums[1].got, full1], [])
-        k_g1 = gate_sums[1].first(got_g, dg1)
-        k_u1 = up_sums[1].first(got_u, du1)
-        dg1, du1, dgot1, full1, k_g1, k_u1, got_g, got_u = tie([dg1, du1, dgot1, full1, k_g1, k_u1, gate_sums[0].got, up_sums[0].got], [gate_sums[1].sent, up_sums[1].sent])
+        full1, dgot1, got_g, got_u = tie([full1, dgot1, gate_sums[0].got, up_sums[0].got], [c_g1, c_u1])
+        dsent1, dkept1, dgot1x = down_x(full1, dgot1)
         t_g0 = gate_sums[0].third(got_g, gate_sums[0].kept)
         t_u0 = up_sums[0].third(got_u, up_sums[0].kept)
-        dsent1, dkept1, dgot1x = down_x(full1, dgot1)
-        dg1, du1, d_mid = tie([dg1, du1, d_mid], [t_g0, t_u0, dsent1, dkept1])
-        d_mid = round_bf(d_mid + dot_nt(dg1, wg1) + dot_nt(du1, wu1))
+        dg1, du1, got_g, got_u = tie([dg1, du1, gate_sums[1].got, up_sums[1].got], [dsent1, dkept1, t_g0, t_u0])
+        k_u1 = up_sums[1].first(got_u, du1)
+        k_g1 = gate_sums[1].first(got_g, dg1)
+        dg1, du1, d_mid = tie([dg1, du1, d_mid], [k_g1, k_u1, gate_sums[1].sent, up_sums[1].sent])
+        d_mid = d_mid + dot_nt(dg1, wg1)
+        d_mid, du1, dkept0, dkept1, dgot0x, dgot1x = tie([d_mid, du1, dkept0, dkept1, dgot0x, dgot1x], [])
+        low = spot.y == 0
+        down_sent = bf16(jnp.where(low, dkept1 + f32(dgot1x), dkept0 + f32(dgot0x)))
+        down_kept = jnp.where(low, dkept0 + f32(dgot0x), dkept1 + f32(dgot1x))
+        down_got = swap(down_sent, 4)
+        d_mid, du1 = tie([d_mid, du1], [down_sent, down_kept])
+        d_mid = round_bf(d_mid + dot_nt(du1, wu1))
 
         d_resid_norm, sum_norm_mlp = rms_back(d_mid, resid_f, inv_mid, gain_mid)
         d_resid = bf16(f32(grad_y) + d_resid_norm)
-        d_resid, dkept0, dkept1, dgot0x, k_g1, k_u1, got_g, got_u = tie([d_resid, dkept0, dkept1, dgot0x, k_g1, k_u1, gate_sums[1].got, up_sums[1].got], [])
-        s_g1 = gate_sums[1].second(got_g, k_g1)
+        d_resid, k_u1, got_u = tie([d_resid, k_u1, up_sums[1].got], [])
         s_u1 = up_sums[1].second(got_u, k_u1)
         o_cut = width // 2
         o_sums = [WeightSum(spot, o_parts, first, rows) for first in (True, False)]
         c_o = [o_sums[i].core(d_resid[:, i * o_cut:(i + 1) * o_cut]) for i in range(2)]
-        d_res_m, dgot1x = tie([d_resid, dgot1x], c_o + [s_g1, s_u1])
-        low = spot.y == 0
-        down_sent = bf16(jnp.where(low, dkept1 + f32(dgot1x), dkept0 + f32(dgot0x)))
-        down_kept = jnp.where(low, dkept0 + f32(dgot0x), dkept1 + f32(dgot1x))
-        down_got = swap(down_sent, 4)
+        d_res_m, = tie([d_resid], c_o + [s_u1])
         d_attn = bf16(dot_nt(d_res_m, wo))
-        d_attn, got_g, got_u, got_o0, got_o1 = tie([d_attn, gate_sums[1].got, up_sums[1].got, o_sums[0].got, o_sums[1].got], [down_sent, down_kept])
+        d_attn, k_g1, got_g, got_o0, got_o1 = tie([d_attn, k_g1, gate_sums[1].got, o_sums[0].got, o_sums[1].got], [])
+        s_g1 = gate_sums[1].second(got_g, k_g1)
         k_o = [o_sums[i].first(got, d_resid[:, i * o_cut:(i + 1) * o_cut]) for i, got in enumerate((got_o0, got_o1))]
-        t_g1 = gate_sums[1].third(got_g, gate_sums[1].kept)
-        t_u1 = up_sums[1].third(got_u, up_sums[1].kept)
-        d_attn, = tie([d_attn], k_o + [t_g1, t_u1, o_sums[0].sent, o_sums[1].sent])
-        d_q, d_k, d_v, sum_bq, sum_bk, sum_bv = attention_bwd(q_rot, k_rot, v_all, d_attn, cos_t, sin_t, start_row)
-        d_qkv = jnp.concatenate([d_q, d_k, d_v], axis=1)
-        d_qkv, k_o0, k_o1, got_o0, got_o1, down_got, down_kept = tie([d_qkv] + k_o + [o_sums[0].got, o_sums[1].got, down_got, down_kept], [])
-        s_o = [o_sums[0].second(got_o0, k_o0), o_sums[1].second(got_o1, k_o1)]
+        d_attn, = tie([d_attn], k_o + [s_g1, o_sums[0].sent, o_sums[1].sent])
+        grads_a = attention_bwd(0, q_rot, k_rot, v_all, d_attn, cos_t, sin_t, start_row)
+        held = tie(list(grads_a) + k_o + [d_attn, o_sums[0].got, o_sums[1].got, down_got, down_kept, up_sums[1].got], [])
+        grads_a, (k_o0, k_o1, d_attn, got_o0, got_o1, down_got, down_kept, got_u) = held[:6], held[6:]
         down_mine = bf16(down_kept + f32(down_got))
         down_rep = swap_rep(down_mine)
+        t_u1 = up_sums[1].third(got_u, up_sums[1].kept)
+        s_o = [o_sums[0].second(got_o0, k_o0), o_sums[1].second(got_o1, k_o1)]
+        d_attn, = tie([d_attn], s_o + [down_mine, t_u1])
+        grads_b = attention_bwd(1, q_rot, k_rot, v_all, d_attn, cos_t, sin_t, start_row)
+        d_qkv = jnp.concatenate([grads_a[0], grads_b[0], grads_a[1], grads_b[1], grads_a[2], grads_b[2]], axis=1)
+        sum_bq, sum_bk, sum_bv = [jnp.concatenate([grads_a[i][0], grads_b[i][0]]) for i in (3, 4, 5)]
+        d_qkv, got_g, got_o0, got_o1 = tie([d_qkv, gate_sums[1].got, o_sums[0].got, o_sums[1].got], [])
         q_cut = d_qkv.shape[1] // 2
         q_sums = [WeightSum(spot, in_parts, first, rows) for first in (True, False)]
         c_q = [q_sums[i].core(d_qkv[:, i * q_cut:(i + 1) * q_cut]) for i in range(2)]
-        d_qkv, got_q0, got_q1 = tie([d_qkv, q_sums[0].got, q_sums[1].got], s_o + c_q + [down_mine])
+        t_g1 = gate_sums[1].third(got_g, gate_sums[1].kept)
+        t_o = [o_sums[0].third(got_o0, o_sums[0].kept), o_sums[1].third(got_o1, o_sums[1].kept)]
+        d_qkv, got_q0, got_q1 = tie([d_qkv, q_sums[0].got, q_sums[1].got], c_q + t_o + [t_g1])
         k_q = [q_sums[i].first(got, d_qkv[:, i * q_cut:(i + 1) * q_cut]) for i, got in enumerate((got_q0, got_q1))]
-        d_qkv, got_o0, got_o1 = tie([d_qkv, o_sums[0].got, o_sums[1].got], k_q + [q_sums[0].sent, q_sums[1].sent])
-        t_o = [o_sums[0].third(got_o0, o_sums[0].kept), o_sums[1].third(got_o1, o_sums[1].kept)]
-        d_qkv, = tie([d_qkv], t_o)
+        d_qkv, = tie([d_qkv], k_q + [q_sums[0].sent, q_sums[1].sent])
         d_normed_in = round_bf(dot_nt(d_qkv, wqkv))
         d_x_norm, sum_norm_attn = rms_back(d_normed_in, x_f, inv_in, gain_in)
+        sum_norm_attn, = tie([sum_norm_attn], [])
+        k_q0, k_q1, got_q0, got_q1 = tie(k_q + [q_sums[0].got, q_sums[1].got], [sum_norm_attn])
+        s_q = [q_sums[0].second(got_q0, k_q0), q_sums[1].second(got_q1, k_q1)]
+        d_resid, d_x_norm = tie([d_resid, d_x_norm], s_q)
         grad_x = bf16(f32(d_resid) + d_x_norm)
-        k_q0, k_q1, got_q0, got_q1, grad_x, sum_norm_attn = tie(k_q + [q_sums[0].got, q_sums[1].got, grad_x, sum_norm_attn], [])
-        s_q = [q_sums[0].second(got_q0, k_q0), q_sums[1].second(got_q1, k_q1)]
-        sum_norm_attn, = tie([sum_norm_attn], s_q)
-
-        vecs = [sum_bq[0], sum_bk[0], sum_bv[0], sum_norm_attn, sum_norm_mlp]
+
+        vecs = [sum_bq, sum_bk, sum_bv, sum_norm_attn, sum_norm_mlp]
         flat = stack_rows([v.reshape(8, 1, -1) for v in vecs])
-        flat = pick(lax.psum(flat, ('rep', 'shard')), lax.axis_index('shard'), 0) * inv_count
+        flat = lax.psum(flat, ('rep', 'shard'))
+        t_q = [part.third(part.got, part.kept) for part in q_sums]
+        late = [gate_sums[1], up_sums[1]] + o_sums
+        ends = tie([part.got for part in late] + [down_rep, flat], t_q)
+        for part, got in zip(late, ends):
+            part.got = got
+        down_rep, flat = ends[-2:]
+        flat = pick(flat, lax.axis_index('shard'), 0) * inv_count
         vec_out = [flat[i, :n] for i, n in enumerate(sizes)]
-        for part in q_sums:
-            part.third(part.got, part.kept)
 
         def joined(parts):
             return jnp.concatenate([part.result() for part in parts], axis=1) * inv_count

time: 1380 us -> 1350 us (0.978)
  waiting for transfers between devices: 261 us -> 220 us
  matrix products: 656 us -> 618 us
  local copies, waits for them, and re-layouts: 97 us -> 128 us
  other arithmetic: 152 us -> 170 us
    psum x1, waiting for transfers between devices: 52.3 us -> 0.01 us  [per_device(): flat = lax.psum(flat, ('rep', 'shard'))]
    slice x2 -> x20, local copies, waits for them, and re-layouts: 0.04 us -> 51.6 us  [the longest x8 28.7 us: first(): self.kept = own[2 * self.rows:]]
    ppermute x9, waiting for transfers between devices: 40.6 us -> 79.6 us  [swap_rep(): return lax.ppermute(arr, 'rep', [(0, 1), (1, 0)])]
    dot_general x30 -> x22, matrix products: 373 us -> 336 us  [dot_nn(): lax.dot_general(a, b, (((1,), (0,)), ((), ())), preferred_element_type=jn...]
    dynamic_slice x17 -> x3, local copies, waits for them, and re-layouts: 37.3 us -> 5.49 us  [pick(): return lax.dynamic_index_in_dim(arr, index, axis, keepdims=False)]
    ppermute x29, waiting for transfers between devices: 71.4 us -> 49.7 us  [swap(): return lax.ppermute(arr, 'shard', [(s, s ^ bit) for s in range(8)])]
    another operation x0 -> x12, other arithmetic: none -> 20.1 us  [split_rows(): jnp.stack([pick(mine, 1 - here, axis), pick(mine, here, axis)])]
    unnamed x177 -> x198, local copies, waits for them, and re-layouts: 24.1 us -> 33.7 us
  transfers between devices with their start and end apart: 46 -> 46, of which waited for: 10 -> 10; matrix products, arithmetic and copies ran while one was open for 64% -> 63% of each run, Pallas kernels for 11% -> 11%
where the time goes in v2:
time: 1350 us; the launch traced here: 1340 us
  matrix products  618 us (46%)
  waiting for transfers between devices  220 us (16%)
  other arithmetic  170 us (13%)
  Pallas kernels  142 us (11%)
  local copies, waits for them, and re-layouts  128 us (9%)
  starting transfers between devices  34.2 us (3%)
  between operations  16.8 us (1%)
    dot_general x22, matrix products, dot_nn(): lax.dot_general(a, b, (((1,), (0,)), ((), ())), preferred_element_type=jn...  336 us
    dot_general x8, matrix products, dot_nt(): lax.dot_general(a, b, (((1,), (1,)), ((), ())), preferred_element_type=jn...  227 us
    all_gather x7, waiting for transfers between devices, gather(): return lax.all_gather(part, 'shard', axis=0, tiled=True)  87.7 us
    pallas_call x2, Pallas kernels, attention_bwd(): pl.pallas_call(attn_bwd_kernel, grid=(GROUP,), in_specs=[q_in, kv_in, kv_...  81.3 us
    ppermute x9, waiting for transfers between devices, swap_rep(): return lax.ppermute(arr, 'rep', [(0, 1), (1, 0)])  79.6 us
    convert_element_type x20, other arithmetic, bf16(): return arr.astype(jnp.bfloat16)  65.1 us
    pallas_call x1, Pallas kernels, attention_fwd(): pl.pallas_call(attn_fwd_kernel, grid=(HEADS,), in_specs=[head_spec(tokens...  61.1 us
    dot_general x2, matrix products, dot_tn(): lax.dot_general(a, b, (((0,), (0,)), ((), ())), preferred_element_type=jn...  54.9 us
  transfers between devices with their start and end apart: 46, of which 10 were waited for; matrix products, arithmetic and copies ran while one was open for 63% of the time, Pallas kernels for 11%

profile of v2, /device:TPU:0, one launch (start us, length us, event | category | flops | bytes accessed | tf_op | source)
XLA Modules:
  0.0 1340.2 jit_solution(1024261922140285608)
XLA Ops:
  56.2 16.6 %convolution_add_fusion.3.q_in.k_in.v_in = f32[1536,2048]{1,0:T(8,128)} fusion(bf16[1536,1536]{0,1:T(8,128)(2,1)} %copy-done.9, bf16[1536,2048]{1,0:T(8,128)(2,1)} %all-gather.9.cloned.1.call-done, f32[2048]{0:T(1024)S(1)} %pad_maximum_fusion.15), kind=kOutput, calls=%fused_computation.68 | convolution fusion | flops 9666822144 | bytes 23601152 | tf_op jit(solution)/shard_map/dot_general | solution.py:30
  72.8 61.1 %attn_fwd.1 = (bf16[1536,1536]{1,0:T(8,128)(2,1)}, bf16[1536,256]{1,0:T(8,128)(2,1)S(1)}, bf16[1536,256]{1,0:T(8,128)(2,1)S(1)}, bf16[1536,1536]{1,0:T(8,128)(2,1)}) custom-call(f32[1536,2048]{1,0:T(8,128)} %convolution_add_fusion.3.q_in.k_in.v_in, f32[1536,2048]{1,0:T(8,128)} %convolution_add_fusion.3.q_in.k_in.v_in, ...), custom_call_target="tpu_custom_call" | custom-call | flops 34789236736 | bytes 30000000 | tf_op jit(solution)/shard_map/attn_fwd/pallas_call | solution.py:140
  180.4 30.6 %fusion.96 = f32[1536,4480]{1,0:T(8,128)} fusion(bf16[1536,1536]{0,1:T(8,128)(2,1)} %copy-done.8, bf16[1536,4480]{1,0:T(8,128)(2,1)} %all-gather.15.cloned.1.call-done), kind=kOutput, calls=%fused_computation.248 | convolution fusion | flops 21139292160 | bytes 46006272 | tf_op jit(solution)/shard_map/dot_general | solution.py:30
  211.1 31.1 %all-gather.17.cloned.1.call-done = bf16[1536,4480]{1,0:T(8,128)(2,1)} async-done(((bf16[192,4480]{1,0:T(8,128)(2,1)}), bf16[1536,4480]{1,0:T(8,128)(2,1)}) %all-gather.17.cloned.1.call-update) | async-done | bytes 13762576 | tf_op jit(solution)/shard_map/all_gather | solution.py:296
  242.1 39.5 %multiply_convert_fusion.1 = (bf16[1536,4480]{1,0:T(8,128)(2,1)}, f32[1536,4480]{1,0:T(8,128)}) fusion(f32[1536,4480]{1,0:T(8,128)} %fusion.96, bf16[1536,1536]{0,1:T(8,128)(2,1)} %copy-done.8, bf16[1536,4480]{1,0:T(8,128)(2,1)} %all-gather.17.cloned.1.call-done), kind=kOutput, calls=%fused_computation.16 | convolution fusion | flops 21180579840 | bytes 87293952 | tf_op jit(solution)/shard_map/dot_general | solution.py:30
  281.6 28.1 %fusion.97 = f32[4480,1536]{1,0:T(8,128)} fusion(bf16[1536,4480]{1,0:T(8,128)(2,1)} %get-tuple-element.141, bf16[1536,1536]{1,0:T(8,128)(2,1)} %param.19), kind=kOutput, calls=%fused_computation.249 | convolution fusion | flops 21139292160 | bytes 46006272 | tf_op jit(solution)/shard_map/dot_general | solution.py:38
  318.6 56.6 %all-gather.13.cloned.1.call-done = bf16[8960,1536]{1,0:T(8,128)(2,1)} async-done(((bf16[1120,1536]{1,0:T(8,128)(2,1)}), bf16[8960,1536]{1,0:T(8,128)(2,1)}) %all-gather.13.cloned.1.call-update) | async-done | bytes 27525136 | tf_op jit(solution)/shard_map/all_gather | solution.py:296
  375.3 49.9 %fusion.7 = (bf16[1536,4480]{1,0:T(8,128)(2,1)}, bf16[1536,4480]{1,0:T(8,128)(2,1)}) fusion(f32[1536,4480]{1,0:T(8,128)} %fusion.96, f32[1536,4480]{1,0:T(8,128)} %get-tuple-element.143, bf16[1536,1536]{1,0:T(8,128)(2,1)} %param.19, bf16[8960,1536]{1,0:T(8,128)(2,1)} %all-gather.13.cloned.1.call-done), kind=kOutput, calls=%fused_computation.11 | convolution fusion | flops 21235630080 | bytes 101056512 | tf_op jit(solution)/shard_map/dot_general | solution.py:34
  425.2 17.0 %convolution_convert_fusion.3 = bf16[768,4480]{1,0:T(8,128)(2,1)} fusion(bf16[768,1536]{1,0:T(8,128)(2,1)} %bitcast.304, bf16[1536,4480]{1,0:T(8,128)(2,1)} %get-tuple-element.160), kind=kOutput, calls=%fused_computation.66 | convolution fusion | flops 10573086720 | bytes 23003136 | tf_op jit(solution)/shard_map/dot_general | solution.py:30
  456.0 14.7 %convert_add_fusion.7 = (f32[1120,1536]{1,0:T(8,128)}, bf16[1120,1536]{1,0:T(8,128)(2,1)}) fusion(f32[2,2,1120,1536]{3,2,1,0:T(8,128)} %bitcast.280, s32[]{:T(128)S(6)} %select_n.158, s32[]{:T(128)S(6)} %select_n.160, bf16[2,1120,1536]{2,1,0:T(8,128)(2,1)} %collective-permute-done, s32[]{:T(128)S(6)} %select_n.157, s32[]{:T(128)S(6)} %select_n.152, ...), kind=kLoop, calls=%fused_computation.81 | loop fusion | flops 8601600 | bytes 30965780 | tf_op jit(solution)/shard_map/add | solution.py:353
  470.6 27.2 %fusion.98 = f32[1536,1536]{0,1:T(8,128)S(1)} fusion(bf16[1536,4480]{1,0:T(8,128)(2,1)} %get-tuple-element.157, bf16[1536,4480]{1,0:T(8,128)(2,1)} %all-gather.15.cloned.1.call-done), kind=kOutput, calls=%fused_computation.250 | convolution fusion | flops 21139292160 | bytes 36962304 | tf_op jit(solution)/shard_map/dot_general | solution.py:34
  497.8 31.1 %convolution_add_fusion.2 = f32[1536,1536]{0,1:T(8,128)} fusion(f32[1536,1536]{0,1:T(8,128)S(1)} %fusion.98, bf16[1536,4480]{1,0:T(8,128)(2,1)} %get-tuple-element.160, bf16[1536,4480]{1,0:T(8,128)(2,1)} %all-gather.17.cloned.1.call-done), kind=kOutput, calls=%fused_computation.41 | convolution fusion | flops 21141651456 | bytes 46399488 | tf_op jit(solution)/shard_map/dot_general | solution.py:34
  529.0 18.2 %convert_add_fusion.3 = f32[768,4480]{1,0:T(8,128)} fusion(bf16[768,4480]{1,0:T(8,128)(2,1)} %collective-permute-done.2, bf16[768,1536]{1,0:T(8,128)(2,1)S(1)} %bitcast.300, bf16[1536,4480]{1,0:T(8,128)(2,1)} %get-tuple-element.160), kind=kOutput, calls=%fused_computation.35 | convolution fusion | flops 10576527360 | bytes 36765696 | tf_op jit(solution)/shard_map/dot_general | solution.py:30
  558.7 18.5 %convert_add_fusion.4 = f32[768,4480]{1,0:T(8,128)} fusion(bf16[768,4480]{1,0:T(8,128)(2,1)} %collective-permute-done.1, bf16[768,1536]{1,0:T(8,128)(2,1)S(1)} %bitcast.302, bf16[1536,4480]{1,0:T(8,128)(2,1)} %get-tuple-element.157), kind=kOutput, calls=%fused_computation.36 | convolution fusion | flops 10576527360 | bytes 36765696 | tf_op jit(solution)/shard_map/dot_general | solution.py:30
  589.4 28.0 %fusion.9 = bf16[1536,4480]{1,0:T(8,128)(2,1)} fusion(bf16[1536,1536]{1,0:T(8,128)(2,1)S(1)} %bitcast.286, bf16[8960,1536]{1,0:T(8,128)(2,1)} %all-gather.13.cloned.1.call-done), kind=kOutput, calls=%fused_computation.29 | convolution fusion | flops 21146173440 | bytes 32243712 | tf_op jit(solution)/shard_map/dot_general | solution.py:34
  617.4 30.5 %fusion.99 = f32[1536,4480]{1,0:T(8,128)} fusion(bf16[1536,1536]{0,1:T(8,128)(2,1)} %copy-done.8, bf16[1536,4480]{1,0:T(8,128)(2,1)} %all-gather.19.cloned.1.call-done), kind=kOutput, calls=%fused_computation.251 | convolution fusion | flops 21139292160 | bytes 46006272 | tf_op jit(solution)/shard_map/dot_general | solution.py:30
  647.9 47.8 %fusion.2 = (bf16[1536,4480]{1,0:T(8,128)(2,1)}, bf16[1536,4480]{1,0:T(8,128)(2,1)}, bf16[1536,4480]{1,0:T(8,128)(2,1)}) fusion(bf16[1536,4480]{1,0:T(8,128)(2,1)} %fusion.9, f32[1536,4480]{1,0:T(8,128)} %fusion.99, bf16[1536,1536]{0,1:T(8,128)(2,1)} %copy-done.8, bf16[1536,4480]{1,0:T(8,128)(2,1)} %all-gather.21.cloned.1.call-done), kind=kOutput, calls=%fused_computation.4 | convolution fusion | flops 21249392640 | bytes 101056512 | tf_op jit(solution)/shard_map/dot_general | solution.py:30
  703.8 26.9 %fusion.100 = f32[4480,1536]{1,0:T(8,128)} fusion(bf16[1536,4480]{1,0:T(8,128)(2,1)} %get-tuple-element.174, bf16[1536,1536]{1,0:T(8,128)(2,1)S(1)} %copy-done.23), kind=kOutput, calls=%fused_computation.252 | convolution fusion | flops 21139292160 | bytes 46006272 | tf_op jit(solution)/shard_map/dot_general | solution.py:38
  739.4 16.9 %convolution_convert_fusion.1 = bf16[768,4480]{1,0:T(8,128)(2,1)} fusion(bf16[768,1536]{1,0:T(8,128)(2,1)} %bitcast.305, bf16[1536,4480]{1,0:T(8,128)(2,1)} %get-tuple-element.196), kind=kOutput, calls=%fused_computation.64 | convolution fusion | flops 10573086720 | bytes 23003136 | tf_op jit(solution)/shard_map/dot_general | solution.py:30
  756.3 16.0 %convolution_convert_fusion.2 = bf16[768,4480]{1,0:T(8,128)(2,1)} fusion(bf16[768,1536]{1,0:T(8,128)(2,1)S(1)} %bitcast.307, bf16[1536,4480]{1,0:T(8,128)(2,1)} %get-tuple-element.187), kind=kOutput, calls=%fused_computation.65 | convolution fusion | flops 10573086720 | bytes 23003136 | tf_op jit(solution)/shard_map/dot_general | solution.py:30
  783.8 29.3 %collective-permute-done.9 = bf16[192,4480]{1,0:T(8,128)(2,1)} collective-permute-done((bf16[192,4480]{1,0:T(8,128)(2,1)}, bf16[192,4480]{1,0:T(8,128)(2,1)}, u32[]{:S(2)}, u32[]{:S(2)}) %collective-permute-start.9) | collective-permute-done | bytes 1720352 | tf_op jit(solution)/shard_map/ppermute | solution.py:202
  834.4 18.1 %convert_add_fusion.1 = f32[768,4480]{1,0:T(8,128)} fusion(bf16[768,4480]{1,0:T(8,128)(2,1)} %collective-permute-done.6, bf16[768,1536]{1,0:T(8,128)(2,1)S(1)} %bitcast.301, bf16[1536,4480]{1,0:T(8,128)(2,1)} %get-tuple-element.196), kind=kOutput, calls=%fused_computation.32 | convolution fusion | flops 10576527360 | bytes 36765696 | tf_op jit(solution)/shard_map/dot_general | solution.py:30
  864.0 18.3 %convert_add_fusion.2 = f32[768,4480]{1,0:T(8,128)} fusion(bf16[768,4480]{1,0:T(8,128)(2,1)} %collective-permute-done.5, bf16[768,1536]{1,0:T(8,128)(2,1)S(1)} %bitcast.303, bf16[1536,4480]{1,0:T(8,128)(2,1)} %get-tuple-element.187), kind=kOutput, calls=%fused_computation.33 | convolution fusion | flops 10576527360 | bytes 36765696 | tf_op jit(solution)/shard_map/dot_general | solution.py:30
  898.6 31.0 %convolution_add_fusion.1 = f32[1536,1536]{0,1:T(8,128)} fusion(f32[1536,1536]{0,1:T(8,128)} %convolution_add_fusion.2, bf16[1536,4480]{1,0:T(8,128)(2,1)} %get-tuple-element.187, bf16[1536,4480]{1,0:T(8,128)(2,1)} %all-gather.19.cloned.1.call-done), kind=kOutput, calls=%fused_computation.40 | convolution fusion | flops 21141651456 | bytes 46399488 | tf_op jit(solution)/shard_map/dot_general | solution.py:34
  940.0 30.2 %collective-permute-done.36 = bf16[192,4480]{1,0:T(8,128)(2,1)S(1)} collective-permute-done((bf16[192,4480]{1,0:T(8,128)(2,1)S(1)}, bf16[192,4480]{1,0:T(8,128)(2,1)S(1)}, u32[]{:S(2)}, u32[]{:S(2)}) %collective-permute-start.36) | collective-permute-done | bytes 1720352 | tf_op jit(solution)/shard_map/ppermute | solution.py:206
  979.7 33.3 %fusion.22 = (f32[1536]{0:T(1024)S(1)}, f32[1536]{0:T(1024)S(1)}, f32[1536,1536]{0,1:T(8,128)}) fusion(bf16[1536,1536]{0,1:T(8,128)(2,1)} %copy-done.11, f32[1536]{0:T(1024)S(1)} %copy-done.58, f32[1536]{0:T(1024)S(1)} %copy-done.62, f32[1536,1536]{0,1:T(8,128)} %convolution_add_fusion.1, bf16[1536,4480]{1,0:T(8,128)(2,1)} %get-tuple-element.196, ...), kind=kOutput, calls=%fused_computation.51 | convolution fusion | flops 21160521728 | bytes 51142656 | tf_op jit(solution)/shard_map/dot_general | solution.py:34
  1032.8 13.5 %convolution_convert_fusion.5.do_ref = bf16[1536,1536]{1,0:T(8,128)(2,1)} fusion(bf16[1536,1536]{0,1:T(8,128)(2,1)} %copy-done.12, bf16[1536,1536]{1,0:T(8,128)(2,1)} %all-gather.11.cloned.1.call-done), kind=kOutput, calls=%fused_computation.69 | convolution fusion | flops 7250116608 | bytes 14155776 | tf_op jit(solution)/shard_map/dot_general | solution.py:34
  1060.1 40.5 %attn_bwd.2 = (bf16[1536,768]{1,0:T(8,128)(2,1)}, bf16[1536,128]{1,0:T(8,128)(2,1)S(1)}, bf16[1536,128]{1,0:T(8,128)(2,1)S(1)}, f32[8,768]{1,0:T(8,128)S(1)}, f3...) custom-call(bf16[1536,1536]{1,0:T(8,128)(2,1)} %get-tuple-element.198.q_ref, bf16[1536,256]{1,0:T(8,128)(2,1)S(1)} %copy-done.3, ...), custom_call_target="tpu_custom_call" | custom-call | flops 32614907904 | bytes 15000000 | tf_op jit(solution)/shard_map/attn_bwd/pallas_call | solution.py:167
  1100.6 20.3 %collective-permute-done.17 = bf16[384,768]{1,0:T(8,128)(2,1)S(1)} collective-permute-done((bf16[384,768]{1,0:T(8,128)(2,1)S(1)}, bf16[384,768]{1,0:T(8,128)(2,1)S(1)}, u32[]{:S(2)}, u32[]{:S(2)}) %collective-permute-start.17) | collective-permute-done | bytes 589856 | tf_op jit(solution)/shard_map/ppermute | solution.py:202
  1140.1 40.8 %attn_bwd.3 = (bf16[1536,768]{1,0:T(8,128)(2,1)}, bf16[1536,128]{1,0:T(8,128)(2,1)S(1)}, bf16[1536,128]{1,0:T(8,128)(2,1)S(1)}, f32[8,768]{1,0:T(8,128)S(1)}, f3...) custom-call(bf16[1536,1536]{1,0:T(8,128)(2,1)} %get-tuple-element.198.q_ref, bf16[1536,256]{1,0:T(8,128)(2,1)S(1)} %copy-done.4, ...), custom_call_target="tpu_custom_call" | custom-call | flops 32614907904 | bytes 15000000 | tf_op jit(solution)/shard_map/attn_bwd/pallas_call | solution.py:167
  1207.8 13.5 %fusion.31 = (f32[1536]{0:T(1024)S(1)}, f32[1536]{0:T(1024)S(1)}, f32[1536,1536]{0,1:T(8,128)}) fusion(bf16[1536,1536]{0,1:T(8,128)(2,1)S(1)} %bitcast.248, f32[1536]{0:T(1024)S(1)} %copy-done.56, f32[1536]{0:T(1024)S(1)} %copy-done.60, bf16[1536,2048]{1,0:T(8,128)(2,1)S(1)} %constant_dynamic-update-slice_fusion, bf16[1536,2048]{1,0:T(8,128)(2,1)S(1)} %bitcast.322), kind=kOutput, calls=%fused_computation.60 | convolution fusion | flops 9682546688 | bytes 26763264 | tf_op jit(solution)/shard_map/dot_general | solution.py:34
  1259.3 30.3 %collective-permute-done.34 = bf16[192,768]{1,0:T(8,128)(2,1)S(1)} collective-permute-done((bf16[192,768]{1,0:T(8,128)(2,1)}, bf16[192,768]{1,0:T(8,128)(2,1)S(1)}, u32[]{:S(2)}, u32[]{:S(2)}) %collective-permute-start.34) | collective-permute-done | bytes 294944 | tf_op jit(solution)/shard_map/ppermute | solution.py:206
  (441 shorter events, 398.0 us)
Async XLA Ops:
  7.2 49.0 %all-gather.9.cloned.1.call-start = ((), (), s32[]{:S(2)}) async-start(), calls=%async_computation | async-start | bytes 7077888 | tf_op jit(solution)/shard_map/all_gather | solution.py:296
  9.4 139.7 %all-gather.11.cloned.1.call-start = ((), (), s32[]{:S(2)}) async-start(), calls=%async_computation.1 | async-start | bytes 5308416 | tf_op jit(solution)/shard_map/all_gather | solution.py:296
  10.2 170.2 %all-gather.15.cloned.1.call-start = ((), (), s32[]{:S(2)}) async-start(), calls=%async_computation.3 | async-start | bytes 15482880 | tf_op jit(solution)/shard_map/all_gather | solution.py:296
  14.4 227.8 %all-gather.17.cloned.1.call-start = ((), (), s32[]{:S(2)}) async-start(), calls=%async_computation.4 | async-start | bytes 15482880 | tf_op jit(solution)/shard_map/all_gather | solution.py:296
  16.5 358.8 %all-gather.13.cloned.1.call-start = ((), (), s32[]{:S(2)}) async-start(), calls=%async_computation.2 | async-start | bytes 30965760 | tf_op jit(solution)/shard_map/all_gather | solution.py:296
  17.1 600.3 %all-gather.19.cloned.1.call-start = ((), (), s32[]{:S(2)}) async-start(), calls=%async_computation.5 | async-start | bytes 15482880 | tf_op jit(solution)/shard_map/all_gather | solution.py:296
  17.7 630.3 %all-gather.21.cloned.1.call-start = ((), (), s32[]{:S(2)}) async-start(), calls=%async_computation.6 | async-start | bytes 15482880 | tf_op jit(solution)/shard_map/all_gather | solution.py:296
  18.4 1279.6 %all-reduce.14.cloned.1.call-start = ((), (), s32[]{:S(2)}) async-start(), calls=%async_computation.7 | async-start | bytes 131072 | tf_op jit(solution)/shard_map/psum | solution.py:454
  318.4 106.8 %collective-permute-start = (bf16[2,1120,1536]{2,1,0:T(8,128)(2,1)}, bf16[2,1120,1536]{2,1,0:T(8,128)(2,1)}, u32[]{:S(2)}, u32[]{:S(2)}) collective-permute-start(bf16[2,1120,1536]{2,1,0:T(8,128)(2,1)} %fusion.33), channel_id=1, source_target_pairs={{0,1},{1,0},{2,3},{3,2},{4,5},{5,4},{6,7},{7,6},{8,9},{9,8},{10,11... | collective-permute-start | bytes 20643848 | tf_op jit(solution)/shard_map/ppermute | solution.py:202
  442.2 86.8 %collective-permute-start.2 = (bf16[768,4480]{1,0:T(8,128)(2,1)}, bf16[768,4480]{1,0:T(8,128)(2,1)}, u32[]{:S(2)}, u32[]{:S(2)}) collective-permute-start(bf16[768,4480]{1,0:T(8,128)(2,1)} %convolution_convert_fusion.3), channel_id=1, source_target_pairs={{0,1},{1,0},{2,3},{3,2},{4,5},{5,4},{6,7},{7,6},{8,9},{9,8},{10,11... | collective-permute-start | bytes 20643848 | tf_op jit(solution)/shard_map/ppermute | solution.py:202
  455.5 73.5 %collective-permute-start.1 = (bf16[768,4480]{1,0:T(8,128)(2,1)}, bf16[768,4480]{1,0:T(8,128)(2,1)}, u32[]{:S(2)}, u32[]{:S(2)}) collective-permute-start(bf16[768,4480]{1,0:T(8,128)(2,1)} %convolution_convert_fusion.4), channel_id=1, source_target_pairs={{0,1},{1,0},{2,3},{3,2},{4,5},{5,4},{6,7},{7,6},{8,9},{9,8},{10,11... | collective-permute-start | bytes 20643848 | tf_op jit(solution)/shard_map/ppermute | solution.py:202
  588.5 107.2 %collective-permute-start.4 = (bf16[384,4480]{1,0:T(8,128)(2,1)}, bf16[384,4480]{1,0:T(8,128)(2,1)}, u32[]{:S(2)}, u32[]{:S(2)}) collective-permute-start(bf16[384,4480]{1,0:T(8,128)(2,1)} %slice.286), channel_id=1, source_target_pairs={{0,4},{1,5},{2,6},{3,7},{4,0},{5,1},{6,2},{7,3},{8,12},{9,13},{10,... | collective-permute-start | bytes 10321928 | tf_op jit(solution)/shard_map/ppermute | solution.py:202
  588.6 107.2 %collective-permute-start.3 = (bf16[384,4480]{1,0:T(8,128)(2,1)}, bf16[384,4480]{1,0:T(8,128)(2,1)}, u32[]{:S(2)}, u32[]{:S(2)}) collective-permute-start(bf16[384,4480]{1,0:T(8,128)(2,1)} %slice.287), channel_id=1, source_target_pairs={{0,2},{1,3},{2,0},{3,1},{4,6},{5,7},{6,4},{7,5},{8,10},{9,11},{10,... | collective-permute-start | bytes 10321928 | tf_op jit(solution)/shard_map/ppermute | solution.py:202
  739.3 74.8 %collective-permute-start.7 = (bf16[2,1120,1536]{2,1,0:T(8,128)(2,1)}, bf16[2,1120,1536]{2,1,0:T(8,128)(2,1)}, u32[]{:S(2)}, u32[]{:S(2)}) collective-permute-start(bf16[2,1120,1536]{2,1,0:T(8,128)(2,1)} %fusion.34), channel_id=1, source_target_pairs={{0,1},{1,0},{2,3},{3,2},{4,5},{5,4},{6,7},{7,6},{8,9},{9,8},{10,11... | collective-permute-start | bytes 20643848 | tf_op jit(solution)/shard_map/ppermute | solution.py:202
  772.3 62.1 %collective-permute-start.6 = (bf16[768,4480]{1,0:T(8,128)(2,1)}, bf16[768,4480]{1,0:T(8,128)(2,1)}, u32[]{:S(2)}, u32[]{:S(2)}) collective-permute-start(bf16[768,4480]{1,0:T(8,128)(2,1)} %convolution_convert_fusion.1), channel_id=1, source_target_pairs={{0,1},{1,0},{2,3},{3,2},{4,5},{5,4},{6,7},{7,6},{8,9},{9,8},{10,11... | collective-permute-start | bytes 20643848 | tf_op jit(solution)/shard_map/ppermute | solution.py:202
  772.8 61.6 %collective-permute-start.5 = (bf16[768,4480]{1,0:T(8,128)(2,1)}, bf16[768,4480]{1,0:T(8,128)(2,1)}, u32[]{:S(2)}, u32[]{:S(2)}) collective-permute-start(bf16[768,4480]{1,0:T(8,128)(2,1)} %convolution_convert_fusion.2), channel_id=1, source_target_pairs={{0,1},{1,0},{2,3},{3,2},{4,5},{5,4},{6,7},{7,6},{8,9},{9,8},{10,11... | collective-permute-start | bytes 20643848 | tf_op jit(solution)/shard_map/ppermute | solution.py:202
  813.1 159.4 %collective-permute-start.10 = (bf16[1120,1536]{1,0:T(8,128)(2,1)}, bf16[1120,1536]{1,0:T(8,128)(2,1)}, u32[]{:S(2)}, u32[]{:S(2)}) collective-permute-start(bf16[1120,1536]{1,0:T(8,128)(2,1)} %get-tuple-element.308), channel_id=1, source_target_pairs={{0,2},{1,3},{2,0},{3,1},{4,6},{5,7},{6,4},{7,5},{8,10},{9,11},{10,... | collective-permute-start | bytes 10321928 | tf_op jit(solution)/shard_map/ppermute | solution.py:202
  893.8 78.7 %collective-permute-start.11 = (bf16[1120,1536]{1,0:T(8,128)(2,1)}, bf16[1120,1536]{1,0:T(8,128)(2,1)}, u32[]{:S(2)}, u32[]{:S(2)}) collective-permute-start(bf16[1120,1536]{1,0:T(8,128)(2,1)} %get-tuple-element.306), channel_id=1, source_target_pairs={{0,2},{1,3},{2,0},{3,1},{4,6},{5,7},{6,4},{7,5},{8,10},{9,11},{10,... | collective-permute-start | bytes 10321928 | tf_op jit(solution)/shard_map/ppermute | solution.py:202
  896.3 74.0 %collective-permute-start.36 = (bf16[192,4480]{1,0:T(8,128)(2,1)S(1)}, bf16[192,4480]{1,0:T(8,128)(2,1)S(1)}, u32[]{:S(2)}, u32[]{:S(2)}) collective-permute-start(bf16[192,4480]{1,0:T(8,128)(2,1)S(1)} %fusion.41), channel_id=1, source_target_pairs={{0,8},{8,0},{1,9},{9,1},{2,10},{10,2},{3,11},{11,3},{4,12},{12,4},... | collective-permute-start | bytes 5160968 | tf_op jit(solution)/shard_map/ppermute | solution.py:206
  896.8 123.5 %collective-permute-start.12 = (bf16[384,4480]{1,0:T(8,128)(2,1)}, bf16[384,4480]{1,0:T(8,128)(2,1)}, u32[]{:S(2)}, u32[]{:S(2)}) collective-permute-start(bf16[384,4480]{1,0:T(8,128)(2,1)} %slice.284), channel_id=1, source_target_pairs={{0,4},{1,5},{2,6},{3,7},{4,0},{5,1},{6,2},{7,3},{8,12},{9,13},{10,... | collective-permute-start | bytes 10321928 | tf_op jit(solution)/shard_map/ppermute | solution.py:202
  935.3 111.1 %collective-permute-start.13 = (bf16[384,4480]{1,0:T(8,128)(2,1)}, bf16[384,4480]{1,0:T(8,128)(2,1)}, u32[]{:S(2)}, u32[]{:S(2)}) collective-permute-start(bf16[384,4480]{1,0:T(8,128)(2,1)} %slice.285), channel_id=1, source_target_pairs={{0,2},{1,3},{2,0},{3,1},{4,6},{5,7},{6,4},{7,5},{8,10},{9,11},{10,... | collective-permute-start | bytes 10321928 | tf_op jit(solution)/shard_map/ppermute | solution.py:202
  1029.9 70.7 %collective-permute-start.19 = (bf16[192,4480]{1,0:T(8,128)(2,1)}, bf16[192,4480]{1,0:T(8,128)(2,1)}, u32[]{:S(2)}, u32[]{:S(2)}) collective-permute-start(bf16[192,4480]{1,0:T(8,128)(2,1)} %fusion.60), channel_id=1, source_target_pairs={{0,2},{1,3},{2,0},{3,1},{4,6},{5,7},{6,4},{7,5},{8,10},{9,11},{10,... | collective-permute-start | bytes 5160968 | tf_op jit(solution)/shard_map/ppermute | solution.py:202
  1030.8 90.2 %collective-permute-start.18 = (bf16[1120,1536]{1,0:T(8,128)(2,1)}, bf16[1120,1536]{1,0:T(8,128)(2,1)}, u32[]{:S(2)}, u32[]{:S(2)}) collective-permute-start(bf16[1120,1536]{1,0:T(8,128)(2,1)} %get-tuple-element.310), channel_id=1, source_target_pairs={{0,4},{1,5},{2,6},{3,7},{4,0},{5,1},{6,2},{7,3},{8,12},{9,13},{10,... | collective-permute-start | bytes 10321928 | tf_op jit(solution)/shard_map/ppermute | solution.py:202
  1054.3 66.7 %collective-permute-start.17 = (bf16[384,768]{1,0:T(8,128)(2,1)S(1)}, bf16[384,768]{1,0:T(8,128)(2,1)S(1)}, u32[]{:S(2)}, u32[]{:S(2)}) collective-permute-start(bf16[384,768]{1,0:T(8,128)(2,1)S(1)} %slice.290), channel_id=1, source_target_pairs={{0,4},{1,5},{2,6},{3,7},{4,0},{5,1},{6,2},{7,3},{8,12},{9,13},{10,... | collective-permute-start | bytes 1769480 | tf_op jit(solution)/shard_map/ppermute | solution.py:202
  1055.0 66.0 %collective-permute-start.16 = (bf16[384,768]{1,0:T(8,128)(2,1)S(1)}, bf16[384,768]{1,0:T(8,128)(2,1)S(1)}, u32[]{:S(2)}, u32[]{:S(2)}) collective-permute-start(bf16[384,768]{1,0:T(8,128)(2,1)S(1)} %slice.291), channel_id=1, source_target_pairs={{0,2},{1,3},{2,0},{3,1},{4,6},{5,7},{6,4},{7,5},{8,10},{9,11},{10,... | collective-permute-start | bytes 1769480 | tf_op jit(solution)/shard_map/ppermute | solution.py:202
  1058.8 125.9 %collective-permute-start.20 = (bf16[192,4480]{1,0:T(8,128)(2,1)}, bf16[192,4480]{1,0:T(8,128)(2,1)}, u32[]{:S(2)}, u32[]{:S(2)}) collective-permute-start(bf16[192,4480]{1,0:T(8,128)(2,1)} %fusion.61), channel_id=1, source_target_pairs={{0,4},{1,5},{2,6},{3,7},{4,0},{5,1},{6,2},{7,3},{8,12},{9,13},{10,... | collective-permute-start | bytes 5160968 | tf_op jit(solution)/shard_map/ppermute | solution.py:202
  1127.7 57.1 %collective-permute-start.22 = (bf16[192,768]{1,0:T(8,128)(2,1)}, bf16[192,768]{1,0:T(8,128)(2,1)S(1)}, u32[]{:S(2)}, u32[]{:S(2)}) collective-permute-start(bf16[192,768]{1,0:T(8,128)(2,1)} %fusion.89), channel_id=1, source_target_pairs={{0,2},{1,3},{2,0},{3,1},{4,6},{5,7},{6,4},{7,5},{8,10},{9,11},{10,... | collective-permute-start | bytes 884744 | tf_op jit(solution)/shard_map/ppermute | solution.py:202
  1129.6 55.2 %collective-permute-start.21 = (bf16[192,768]{1,0:T(8,128)(2,1)}, bf16[192,768]{1,0:T(8,128)(2,1)}, u32[]{:S(2)}, u32[]{:S(2)}) collective-permute-start(bf16[192,768]{1,0:T(8,128)(2,1)} %fusion.88), channel_id=1, source_target_pairs={{0,4},{1,5},{2,6},{3,7},{4,0},{5,1},{6,2},{7,3},{8,12},{9,13},{10,... | collective-permute-start | bytes 884744 | tf_op jit(solution)/shard_map/ppermute | solution.py:202
  1131.3 166.7 %collective-permute-start.32 = (bf16[192,4480]{1,0:T(8,128)(2,1)}, bf16[192,4480]{1,0:T(8,128)(2,1)}, u32[]{:S(2)}, u32[]{:S(2)}) collective-permute-start(bf16[192,4480]{1,0:T(8,128)(2,1)} %fusion.39), channel_id=1, source_target_pairs={{0,8},{8,0},{1,9},{9,1},{2,10},{10,2},{3,11},{11,3},{4,12},{12,4},... | collective-permute-start | bytes 5160968 | tf_op jit(solution)/shard_map/ppermute | solution.py:206
  1139.5 158.5 %collective-permute-start.35 = (bf16[1120,1536]{1,0:T(8,128)(2,1)}, bf16[1120,1536]{1,0:T(8,128)(2,1)}, u32[]{:S(2)}, u32[]{:S(2)}) collective-permute-start(bf16[1120,1536]{1,0:T(8,128)(2,1)} %add_convert_fusion.1), channel_id=1, source_target_pairs={{0,8},{8,0},{1,9},{9,1},{2,10},{10,2},{3,11},{11,3},{4,12},{12,4},... | collective-permute-start | bytes 10321928 | tf_op jit(solution)/shard_map/ppermute | solution.py:206
  1194.1 103.9 %collective-permute-start.31 = (bf16[192,4480]{1,0:T(8,128)(2,1)S(1)}, bf16[192,4480]{1,0:T(8,128)(2,1)}, u32[]{:S(2)}, u32[]{:S(2)}) collective-permute-start(bf16[192,4480]{1,0:T(8,128)(2,1)S(1)} %fusion.38), channel_id=1, source_target_pairs={{0,8},{8,0},{1,9},{9,1},{2,10},{10,2},{3,11},{11,3},{4,12},{12,4},... | collective-permute-start | bytes 5160968 | tf_op jit(solution)/shard_map/ppermute | solution.py:206
  1253.6 42.4 %collective-permute-start.33 = (bf16[192,768]{1,0:T(8,128)(2,1)}, bf16[192,768]{1,0:T(8,128)(2,1)S(1)}, u32[]{:S(2)}, u32[]{:S(2)}) collective-permute-start(bf16[192,768]{1,0:T(8,128)(2,1)} %fusion.85), channel_id=1, source_target_pairs={{0,8},{8,0},{1,9},{9,1},{2,10},{10,2},{3,11},{11,3},{4,12},{12,4},... | collective-permute-start | bytes 884744 | tf_op jit(solution)/shard_map/ppermute | solution.py:206
  (108 other events, 1505.6 us)
Sparse Core Ops, SparseCore 0:
  10.4 44.6 all-gather.8
  57.0 35.0 all-gather.10
  93.9 73.2 all-gather.14
  168.9 73.2 all-gather.16
  243.8 131.4 all-gather.12
  377.0 74.1 all-gather.18
  453.0 73.2 all-gather.20
  1222.2 62.8 all-reduce.13

commit v3 on v2

--- a/solution.py
+++ b/solution.py
@@ -262,13 +262,12 @@
         own, = tie([dot_nn(self.own_acts, grads) + f32(got)], [])
         self.sent = bf16(own[:2 * self.rows])
         self.got = swap(self.sent, self.bit)
-        self.kept = own[2 * self.rows:]
-        return self.kept
+        return own
 
     def second(self, got, kept):
         cols = got.shape[1]
         got = got.reshape(2, self.rows, cols)
-        kept = kept.reshape(2, self.rows, cols)
+        kept = kept[2 * self.rows:].reshape(2, self.rows, cols)
         self.sent = bf16(pick(kept, 1 - self.here2, 0) + f32(pick(got, 1 - self.here2, 0)))
         self.got = swap(self.sent, self.bit2)
         self.kept = pick(kept, self.here2, 0) + f32(pick(got, self.here2, 0))
@@ -391,14 +390,15 @@
         dg1, du1, full1 = tie([dg1, du1, full1], [])
         c_g1 = gate_sums[1].core(dg1)
         c_u1 = up_sums[1].core(du1)
-        full1, dgot1, got_g, got_u = tie([full1, dgot1, gate_sums[0].got, up_sums[0].got], [c_g1, c_u1])
+        full1, dgot1 = tie([full1, dgot1], [c_g1, c_u1])
         dsent1, dkept1, dgot1x = down_x(full1, dgot1)
+        dg1, du1, got_g, got_u = tie([dg1, du1, gate_sums[1].got, up_sums[1].got], [dsent1, dkept1])
+        k_u1 = up_sums[1].first(got_u, du1)
+        k_g1 = gate_sums[1].first(got_g, dg1)
+        dg1, du1, d_mid, got_g, got_u = tie([dg1, du1, d_mid, gate_sums[0].got, up_sums[0].got], [k_g1, k_u1, gate_sums[1].sent, up_sums[1].sent])
         t_g0 = gate_sums[0].third(got_g, gate_sums[0].kept)
         t_u0 = up_sums[0].third(got_u, up_sums[0].kept)
-        dg1, du1, got_g, got_u = tie([dg1, du1, gate_sums[1].got, up_sums[1].got], [dsent1, dkept1, t_g0, t_u0])
-        k_u1 = up_sums[1].first(got_u, du1)
-        k_g1 = gate_sums[1].first(got_g, dg1)
-        dg1, du1, d_mid = tie([dg1, du1, d_mid], [k_g1, k_u1, gate_sums[1].sent, up_sums[1].sent])
+        d_mid, = tie([d_mid], [t_g0, t_u0])
         d_mid = d_mid + dot_nt(dg1, wg1)
         d_mid, du1, dkept0, dkept1, dgot0x, dgot1x = tie([d_mid, du1, dkept0, dkept1, dgot0x, dgot1x], [])
         low = spot.y == 0
@@ -453,7 +453,7 @@
         flat = stack_rows([v.reshape(8, 1, -1) for v in vecs])
         flat = lax.psum(flat, ('rep', 'shard'))
         t_q = [part.third(part.got, part.kept) for part in q_sums]
-        late = [gate_sums[1], up_sums[1]] + o_sums
+        late = gate_sums + up_sums + o_sums
         ends = tie([part.got for part in late] + [down_rep, flat], t_q)
         for part, got in zip(late, ends):
             part.got = got

time: 1350 us -> 1410 us (1.044)
  waiting for transfers between devices: 220 us -> 293 us
    ppermute x29, waiting for transfers between devices: 49.7 us -> 108 us  [swap(): return lax.ppermute(arr, 'shard', [(s, s ^ bit) for s in range(8)])]
    ppermute x9, waiting for transfers between devices: 79.6 us -> 94 us  [swap_rep(): return lax.ppermute(arr, 'rep', [(0, 1), (1, 0)])]
    unnamed x198 -> x216, local copies, waits for them, and re-layouts: 33.7 us -> 32.9 us
  transfers between devices with their start and end apart: 46 -> 46, of which waited for: 10 -> 9; matrix products, arithmetic and copies ran while one was open for 63% -> 57% of each run, Pallas kernels for 11% -> 10%
where the time goes in v3:
time: 1410 us; the launch traced here: 1400 us
  matrix products  622 us (44%)
  waiting for transfers between devices  293 us (21%)
  other arithmetic  167 us (12%)
  Pallas kernels  143 us (10%)
  local copies, waits for them, and re-layouts  120 us (9%)
  starting transfers between devices  31.3 us (2%)
  between operations  16.6 us (1%)
    dot_general x22, matrix products, dot_nn(): lax.dot_general(a, b, (((1,), (0,)), ((), ())), preferred_element_type=jn...  340 us
    dot_general x8, matrix products, dot_nt(): lax.dot_general(a, b, (((1,), (1,)), ((), ())), preferred_element_type=jn...  226 us
    ppermute x29, waiting for transfers between devices, swap(): return lax.ppermute(arr, 'shard', [(s, s ^ bit) for s in range(8)])  108 us
    ppermute x9, waiting for transfers between devices, swap_rep(): return lax.ppermute(arr, 'rep', [(0, 1), (1, 0)])  94 us
    all_gather x7, waiting for transfers between devices, gather(): return lax.all_gather(part, 'shard', axis=0, tiled=True)  88.6 us
    pallas_call x2, Pallas kernels, attention_bwd(): pl.pallas_call(attn_bwd_kernel, grid=(GROUP,), in_specs=[q_in, kv_in, kv_...  81.8 us
    convert_element_type x20, other arithmetic, bf16(): return arr.astype(jnp.bfloat16)  64.7 us
    pallas_call x1, Pallas kernels, attention_fwd(): pl.pallas_call(attn_fwd_kernel, grid=(HEADS,), in_specs=[head_spec(tokens...  61.2 us
  transfers between devices with their start and end apart: 46, of which 9 were waited for; matrix products, arithmetic and copies ran while one was open for 57% of the time, Pallas kernels for 10%

profile of v3, /device:TPU:0, one launch (start us, length us, event | category | flops | bytes accessed | tf_op | source)
XLA Modules:
  0.0 1404.5 jit_solution(11733820800355291505)
XLA Ops:
  56.0 16.3 %convolution_add_fusion.3.q_in.k_in.v_in = f32[1536,2048]{1,0:T(8,128)} fusion(bf16[1536,1536]{0,1:T(8,128)(2,1)} %copy-done.9, bf16[1536,2048]{1,0:T(8,128)(2,1)} %all-gather.9.cloned.1.call-done, f32[2048]{0:T(1024)S(1)} %pad_maximum_fusion.15), kind=kOutput, calls=%fused_computation.68 | convolution fusion | flops 9666822144 | bytes 23601152 | tf_op jit(solution)/shard_map/dot_general | solution.py:30
  72.3 61.2 %attn_fwd.1 = (bf16[1536,1536]{1,0:T(8,128)(2,1)}, bf16[1536,256]{1,0:T(8,128)(2,1)S(1)}, bf16[1536,256]{1,0:T(8,128)(2,1)S(1)}, bf16[1536,1536]{1,0:T(8,128)(2,1)}) custom-call(f32[1536,2048]{1,0:T(8,128)} %convolution_add_fusion.3.q_in.k_in.v_in, f32[1536,2048]{1,0:T(8,128)} %convolution_add_fusion.3.q_in.k_in.v_in, ...), custom_call_target="tpu_custom_call" | custom-call | flops 34789236736 | bytes 30000000 | tf_op jit(solution)/shard_map/attn_fwd/pallas_call | solution.py:140
  179.9 30.4 %fusion.96 = f32[1536,4480]{1,0:T(8,128)} fusion(bf16[1536,1536]{0,1:T(8,128)(2,1)} %copy-done.8, bf16[1536,4480]{1,0:T(8,128)(2,1)} %all-gather.15.cloned.1.call-done), kind=kOutput, calls=%fused_computation.248 | convolution fusion | flops 21139292160 | bytes 46006272 | tf_op jit(solution)/shard_map/dot_general | solution.py:30
  210.3 31.9 %all-gather.17.cloned.1.call-done = bf16[1536,4480]{1,0:T(8,128)(2,1)} async-done(((bf16[192,4480]{1,0:T(8,128)(2,1)}), bf16[1536,4480]{1,0:T(8,128)(2,1)}) %all-gather.17.cloned.1.call-update) | async-done | bytes 13762576 | tf_op jit(solution)/shard_map/all_gather | solution.py:295
  242.2 39.5 %multiply_convert_fusion.1 = (bf16[1536,4480]{1,0:T(8,128)(2,1)}, f32[1536,4480]{1,0:T(8,128)}) fusion(f32[1536,4480]{1,0:T(8,128)} %fusion.96, bf16[1536,1536]{0,1:T(8,128)(2,1)} %copy-done.8, bf16[1536,4480]{1,0:T(8,128)(2,1)} %all-gather.17.cloned.1.call-done), kind=kOutput, calls=%fused_computation.16 | convolution fusion | flops 21180579840 | bytes 87293952 | tf_op jit(solution)/shard_map/dot_general | solution.py:30
  281.7 28.0 %fusion.97 = f32[4480,1536]{1,0:T(8,128)} fusion(bf16[1536,4480]{1,0:T(8,128)(2,1)} %get-tuple-element.144, bf16[1536,1536]{1,0:T(8,128)(2,1)} %param.19), kind=kOutput, calls=%fused_computation.249 | convolution fusion | flops 21139292160 | bytes 46006272 | tf_op jit(solution)/shard_map/dot_general | solution.py:38
  318.7 56.7 %all-gather.13.cloned.1.call-done = bf16[8960,1536]{1,0:T(8,128)(2,1)} async-done(((bf16[1120,1536]{1,0:T(8,128)(2,1)}), bf16[8960,1536]{1,0:T(8,128)(2,1)}) %all-gather.13.cloned.1.call-update) | async-done | bytes 27525136 | tf_op jit(solution)/shard_map/all_gather | solution.py:295
  375.3 49.8 %fusion.7 = (bf16[1536,4480]{1,0:T(8,128)(2,1)}, bf16[1536,4480]{1,0:T(8,128)(2,1)}) fusion(f32[1536,4480]{1,0:T(8,128)} %fusion.96, f32[1536,4480]{1,0:T(8,128)} %get-tuple-element.146, bf16[1536,1536]{1,0:T(8,128)(2,1)} %param.19, bf16[8960,1536]{1,0:T(8,128)(2,1)} %all-gather.13.cloned.1.call-done), kind=kOutput, calls=%fused_computation.11 | convolution fusion | flops 21235630080 | bytes 101056512 | tf_op jit(solution)/shard_map/dot_general | solution.py:34
  425.1 17.0 %convolution_convert_fusion.3 = bf16[768,4480]{1,0:T(8,128)(2,1)} fusion(bf16[768,1536]{1,0:T(8,128)(2,1)} %bitcast.308, bf16[1536,4480]{1,0:T(8,128)(2,1)} %get-tuple-element.163), kind=kOutput, calls=%fused_computation.66 | convolution fusion | flops 10573086720 | bytes 23003136 | tf_op jit(solution)/shard_map/dot_general | solution.py:30
  442.1 13.3 convolution_convert_fusion.4
  455.8 14.9 %convert_add_fusion.7 = (f32[1120,1536]{1,0:T(8,128)}, bf16[1120,1536]{1,0:T(8,128)(2,1)}) fusion(f32[2,2,1120,1536]{3,2,1,0:T(8,128)} %bitcast.280, s32[]{:T(128)S(6)} %select_n.158, s32[]{:T(128)S(6)} %select_n.160, bf16[2,1120,1536]{2,1,0:T(8,128)(2,1)} %collective-permute-done, s32[]{:T(128)S(6)} %select_n.157, s32[]{:T(128)S(6)} %select_n.152, ...), kind=kLoop, calls=%fused_computation.81 | loop fusion | flops 8601600 | bytes 30965780 | tf_op jit(solution)/shard_map/add | solution.py:352
  470.7 27.2 %fusion.98 = f32[1536,1536]{0,1:T(8,128)S(1)} fusion(bf16[1536,4480]{1,0:T(8,128)(2,1)} %get-tuple-element.160, bf16[1536,4480]{1,0:T(8,128)(2,1)} %all-gather.15.cloned.1.call-done), kind=kOutput, calls=%fused_computation.250 | convolution fusion | flops 21139292160 | bytes 36962304 | tf_op jit(solution)/shard_map/dot_general | solution.py:34
  497.9 30.9 %convolution_add_fusion.2 = f32[1536,1536]{0,1:T(8,128)} fusion(f32[1536,1536]{0,1:T(8,128)S(1)} %fusion.98, bf16[1536,4480]{1,0:T(8,128)(2,1)} %get-tuple-element.163, bf16[1536,4480]{1,0:T(8,128)(2,1)} %all-gather.17.cloned.1.call-done), kind=kOutput, calls=%fused_computation.41 | convolution fusion | flops 21141651456 | bytes 46399488 | tf_op jit(solution)/shard_map/dot_general | solution.py:34
  528.8 18.1 %convert_add_fusion.3 = f32[768,4480]{1,0:T(8,128)} fusion(bf16[768,4480]{1,0:T(8,128)(2,1)} %collective-permute-done.2, bf16[768,1536]{1,0:T(8,128)(2,1)S(1)} %bitcast.303, bf16[1536,4480]{1,0:T(8,128)(2,1)} %get-tuple-element.163), kind=kOutput, calls=%fused_computation.35 | convolution fusion | flops 10576527360 | bytes 36765696 | tf_op jit(solution)/shard_map/dot_general | solution.py:30
  552.2 18.3 %convert_add_fusion.4 = f32[768,4480]{1,0:T(8,128)} fusion(bf16[768,4480]{1,0:T(8,128)(2,1)} %collective-permute-done.1, bf16[768,1536]{1,0:T(8,128)(2,1)S(1)} %bitcast.304, bf16[1536,4480]{1,0:T(8,128)(2,1)} %get-tuple-element.160), kind=kOutput, calls=%fused_computation.36 | convolution fusion | flops 10576527360 | bytes 36765696 | tf_op jit(solution)/shard_map/dot_general | solution.py:30
  576.5 28.1 %fusion.9 = bf16[1536,4480]{1,0:T(8,128)(2,1)} fusion(bf16[1536,1536]{1,0:T(8,128)(2,1)S(1)} %bitcast.286, bf16[8960,1536]{1,0:T(8,128)(2,1)} %all-gather.13.cloned.1.call-done), kind=kOutput, calls=%fused_computation.29 | convolution fusion | flops 21146173440 | bytes 32243712 | tf_op jit(solution)/shard_map/dot_general | solution.py:34
  604.5 30.4 %fusion.99 = f32[1536,4480]{1,0:T(8,128)} fusion(bf16[1536,1536]{0,1:T(8,128)(2,1)} %copy-done.8, bf16[1536,4480]{1,0:T(8,128)(2,1)} %all-gather.19.cloned.1.call-done), kind=kOutput, calls=%fused_computation.251 | convolution fusion | flops 21139292160 | bytes 46006272 | tf_op jit(solution)/shard_map/dot_general | solution.py:30
  634.9 48.1 %fusion.2 = (bf16[1536,4480]{1,0:T(8,128)(2,1)}, bf16[1536,4480]{1,0:T(8,128)(2,1)}, bf16[1536,4480]{1,0:T(8,128)(2,1)}) fusion(bf16[1536,4480]{1,0:T(8,128)(2,1)} %fusion.9, f32[1536,4480]{1,0:T(8,128)} %fusion.99, bf16[1536,1536]{0,1:T(8,128)(2,1)} %copy-done.8, bf16[1536,4480]{1,0:T(8,128)(2,1)} %all-gather.21.cloned.1.call-done), kind=kOutput, calls=%fused_computation.4 | convolution fusion | flops 21249392640 | bytes 101056512 | tf_op jit(solution)/shard_map/dot_general | solution.py:30
  698.7 27.5 %fusion.100 = f32[4480,1536]{1,0:T(8,128)} fusion(bf16[1536,4480]{1,0:T(8,128)(2,1)} %get-tuple-element.177, bf16[1536,1536]{1,0:T(8,128)(2,1)S(1)} %bitcast.288), kind=kOutput, calls=%fused_computation.252 | convolution fusion | flops 21139292160 | bytes 46006272 | tf_op jit(solution)/shard_map/dot_general | solution.py:38
  734.7 16.9 %convolution_convert_fusion.1 = bf16[768,4480]{1,0:T(8,128)(2,1)} fusion(bf16[768,1536]{1,0:T(8,128)(2,1)} %bitcast.309, bf16[1536,4480]{1,0:T(8,128)(2,1)} %get-tuple-element.200), kind=kOutput, calls=%fused_computation.64 | convolution fusion | flops 10573086720 | bytes 23003136 | tf_op jit(solution)/shard_map/dot_general | solution.py:30
  752.1 16.2 %convolution_convert_fusion.2 = bf16[768,4480]{1,0:T(8,128)(2,1)} fusion(bf16[768,1536]{1,0:T(8,128)(2,1)S(1)} %bitcast.307, bf16[1536,4480]{1,0:T(8,128)(2,1)} %get-tuple-element.191), kind=kOutput, calls=%fused_computation.65 | convolution fusion | flops 10573086720 | bytes 23003136 | tf_op jit(solution)/shard_map/dot_general | solution.py:30
  793.9 18.8 %convert_add_fusion.1 = f32[768,4480]{1,0:T(8,128)} fusion(bf16[768,4480]{1,0:T(8,128)(2,1)} %collective-permute-done.6, bf16[768,1536]{1,0:T(8,128)(2,1)} %bitcast.302, bf16[1536,4480]{1,0:T(8,128)(2,1)} %get-tuple-element.200), kind=kOutput, calls=%fused_computation.32 | convolution fusion | flops 10576527360 | bytes 36765696 | tf_op jit(solution)/shard_map/dot_general | solution.py:30
  818.0 18.7 %convert_add_fusion.2 = f32[768,4480]{1,0:T(8,128)} fusion(bf16[768,4480]{1,0:T(8,128)(2,1)} %collective-permute-done.5, bf16[768,1536]{1,0:T(8,128)(2,1)S(1)} %bitcast.305, bf16[1536,4480]{1,0:T(8,128)(2,1)} %get-tuple-element.191), kind=kOutput, calls=%fused_computation.33 | convolution fusion | flops 10576527360 | bytes 36765696 | tf_op jit(solution)/shard_map/dot_general | solution.py:30
  841.9 48.3 %collective-permute-done.9 = bf16[192,4480]{1,0:T(8,128)(2,1)} collective-permute-done((bf16[192,4480]{1,0:T(8,128)(2,1)}, bf16[192,4480]{1,0:T(8,128)(2,1)}, u32[]{:S(2)}, u32[]{:S(2)}) %collective-permute-start.9) | collective-permute-done | bytes 1720352 | tf_op jit(solution)/shard_map/ppermute | solution.py:202
  900.1 31.2 %convolution_add_fusion.1 = f32[1536,1536]{0,1:T(8,128)} fusion(f32[1536,1536]{0,1:T(8,128)} %convolution_add_fusion.2, bf16[1536,4480]{1,0:T(8,128)(2,1)} %get-tuple-element.191, bf16[1536,4480]{1,0:T(8,128)(2,1)} %all-gather.19.cloned.1.call-done), kind=kOutput, calls=%fused_computation.40 | convolution fusion | flops 21141651456 | bytes 46399488 | tf_op jit(solution)/shard_map/dot_general | solution.py:34
  931.3 32.6 %collective-permute-done.11 = bf16[1120,1536]{1,0:T(8,128)(2,1)} collective-permute-done((bf16[1120,1536]{1,0:T(8,128)(2,1)}, bf16[1120,1536]{1,0:T(8,128)(2,1)}, u32[]{:S(2)}, u32[]{:S(2)}) %collective-permute-start.11) | collective-permute-done | bytes 3440672 | tf_op jit(solution)/shard_map/ppermute | solution.py:202
  971.1 33.1 %fusion.22 = (f32[1536]{0:T(1024)S(1)}, f32[1536]{0:T(1024)S(1)}, f32[1536,1536]{0,1:T(8,128)}) fusion(bf16[1536,1536]{0,1:T(8,128)(2,1)} %copy-done.16, f32[1536]{0:T(1024)S(1)} %copy-done.67, f32[1536]{0:T(1024)S(1)} %copy-done.71, f32[1536,1536]{0,1:T(8,128)} %convolution_add_fusion.1, bf16[1536,4480]{1,0:T(8,128)(2,1)} %get-tuple-element.200, ...), kind=kOutput, calls=%fused_computation.51 | convolution fusion | flops 21160521728 | bytes 51142656 | tf_op jit(solution)/shard_map/dot_general | solution.py:34
  1058.5 40.7 %attn_bwd.2 = (bf16[1536,768]{1,0:T(8,128)(2,1)}, bf16[1536,128]{1,0:T(8,128)(2,1)S(1)}, bf16[1536,128]{1,0:T(8,128)(2,1)S(1)}, f32[8,768]{1,0:T(8,128)S(1)}, f3...) custom-call(bf16[1536,1536]{1,0:T(8,128)(2,1)} %get-tuple-element.202.q_ref, bf16[1536,256]{1,0:T(8,128)(2,1)S(1)} %copy-done.3, ...), custom_call_target="tpu_custom_call" | custom-call | flops 32614907904 | bytes 15000000 | tf_op jit(solution)/shard_map/attn_bwd/pallas_call | solution.py:167
  1100.4 27.4 %collective-permute-done.17 = bf16[384,768]{1,0:T(8,128)(2,1)S(1)} collective-permute-done((bf16[384,768]{1,0:T(8,128)(2,1)S(1)}, bf16[384,768]{1,0:T(8,128)(2,1)S(1)}, u32[]{:S(2)}, u32[]{:S(2)}) %collective-permute-start.17) | collective-permute-done | bytes 589856 | tf_op jit(solution)/shard_map/ppermute | solution.py:202
  1145.6 41.1 %attn_bwd.3 = (bf16[1536,768]{1,0:T(8,128)(2,1)}, bf16[1536,128]{1,0:T(8,128)(2,1)S(1)}, bf16[1536,128]{1,0:T(8,128)(2,1)S(1)}, f32[8,768]{1,0:T(8,128)S(1)}, f3...) custom-call(bf16[1536,1536]{1,0:T(8,128)(2,1)} %get-tuple-element.202.q_ref, bf16[1536,256]{1,0:T(8,128)(2,1)S(1)} %copy-done.4, ...), custom_call_target="tpu_custom_call" | custom-call | flops 32614907904 | bytes 15000000 | tf_op jit(solution)/shard_map/attn_bwd/pallas_call | solution.py:167
  1215.1 13.5 fusion.31
  1270.0 78.8 %collective-permute-done.36 = bf16[192,768]{1,0:T(8,128)(2,1)S(1)} collective-permute-done((bf16[192,768]{1,0:T(8,128)(2,1)}, bf16[192,768]{1,0:T(8,128)(2,1)S(1)}, u32[]{:S(2)}, u32[]{:S(2)}) %collective-permute-start.36) | collective-permute-done | bytes 294944 | tf_op jit(solution)/shard_map/ppermute | solution.py:206
  (460 shorter events, 383.2 us)
Async XLA Ops:
  9.4 139.2 %all-gather.11.cloned.1.call-start = ((), (), s32[]{:S(2)}) async-start(), calls=%async_computation.1 | async-start | bytes 5308416 | tf_op jit(solution)/shard_map/all_gather | solution.py:295
  10.2 169.7 %all-gather.15.cloned.1.call-start = ((), (), s32[]{:S(2)}) async-start(), calls=%async_computation.3 | async-start | bytes 15482880 | tf_op jit(solution)/shard_map/all_gather | solution.py:295
  14.5 227.7 %all-gather.17.cloned.1.call-start = ((), (), s32[]{:S(2)}) async-start(), calls=%async_computation.4 | async-start | bytes 15482880 | tf_op jit(solution)/shard_map/all_gather | solution.py:295
  16.6 358.7 %all-gather.13.cloned.1.call-start = ((), (), s32[]{:S(2)}) async-start(), calls=%async_computation.2 | async-start | bytes 30965760 | tf_op jit(solution)/shard_map/all_gather | solution.py:295
  17.2 587.3 %all-gather.19.cloned.1.call-start = ((), (), s32[]{:S(2)}) async-start(), calls=%async_computation.5 | async-start | bytes 15482880 | tf_op jit(solution)/shard_map/all_gather | solution.py:295
  17.8 617.1 %all-gather.21.cloned.1.call-start = ((), (), s32[]{:S(2)}) async-start(), calls=%async_computation.6 | async-start | bytes 15482880 | tf_op jit(solution)/shard_map/all_gather | solution.py:295
  18.5 1338.8 %all-reduce.14.cloned.1.call-start = ((), (), s32[]{:S(2)}) async-start(), calls=%async_computation.7 | async-start | bytes 131072 | tf_op jit(solution)/shard_map/psum | solution.py:454
  318.4 106.7 %collective-permute-start = (bf16[2,1120,1536]{2,1,0:T(8,128)(2,1)}, bf16[2,1120,1536]{2,1,0:T(8,128)(2,1)}, u32[]{:S(2)}, u32[]{:S(2)}) collective-permute-start(bf16[2,1120,1536]{2,1,0:T(8,128)(2,1)} %fusion.33), channel_id=1, source_target_pairs={{0,1},{1,0},{2,3},{3,2},{4,5},{5,4},{6,7},{7,6},{8,9},{9,8},{10,11... | collective-permute-start | bytes 20643848 | tf_op jit(solution)/shard_map/ppermute | solution.py:202
  442.0 86.8 %collective-permute-start.2 = (bf16[768,4480]{1,0:T(8,128)(2,1)}, bf16[768,4480]{1,0:T(8,128)(2,1)}, u32[]{:S(2)}, u32[]{:S(2)}) collective-permute-start(bf16[768,4480]{1,0:T(8,128)(2,1)} %convolution_convert_fusion.3), channel_id=1, source_target_pairs={{0,1},{1,0},{2,3},{3,2},{4,5},{5,4},{6,7},{7,6},{8,9},{9,8},{10,11... | collective-permute-start | bytes 20643848 | tf_op jit(solution)/shard_map/ppermute | solution.py:202
  455.3 73.5 %collective-permute-start.1 = (bf16[768,4480]{1,0:T(8,128)(2,1)}, bf16[768,4480]{1,0:T(8,128)(2,1)}, u32[]{:S(2)}, u32[]{:S(2)}) collective-permute-start(bf16[768,4480]{1,0:T(8,128)(2,1)} %convolution_convert_fusion.4), channel_id=1, source_target_pairs={{0,1},{1,0},{2,3},{3,2},{4,5},{5,4},{6,7},{7,6},{8,9},{9,8},{10,11... | collective-permute-start | bytes 20643848 | tf_op jit(solution)/shard_map/ppermute | solution.py:202
  575.6 107.4 %collective-permute-start.4 = (bf16[384,4480]{1,0:T(8,128)(2,1)}, bf16[384,4480]{1,0:T(8,128)(2,1)}, u32[]{:S(2)}, u32[]{:S(2)}) collective-permute-start(bf16[384,4480]{1,0:T(8,128)(2,1)} %slice.278), channel_id=1, source_target_pairs={{0,4},{1,5},{2,6},{3,7},{4,0},{5,1},{6,2},{7,3},{8,12},{9,13},{10,... | collective-permute-start | bytes 10321928 | tf_op jit(solution)/shard_map/ppermute | solution.py:202
  575.6 107.4 %collective-permute-start.3 = (bf16[384,4480]{1,0:T(8,128)(2,1)}, bf16[384,4480]{1,0:T(8,128)(2,1)}, u32[]{:S(2)}, u32[]{:S(2)}) collective-permute-start(bf16[384,4480]{1,0:T(8,128)(2,1)} %slice.279), channel_id=1, source_target_pairs={{0,2},{1,3},{2,0},{3,1},{4,6},{5,7},{6,4},{7,5},{8,10},{9,11},{10,... | collective-permute-start | bytes 10321928 | tf_op jit(solution)/shard_map/ppermute | solution.py:202
  775.7 155.6 %collective-permute-start.10 = (bf16[1120,1536]{1,0:T(8,128)(2,1)}, bf16[1120,1536]{1,0:T(8,128)(2,1)}, u32[]{:S(2)}, u32[]{:S(2)}) collective-permute-start(bf16[1120,1536]{1,0:T(8,128)(2,1)} %get-tuple-element.314), channel_id=1, source_target_pairs={{0,2},{1,3},{2,0},{3,1},{4,6},{5,7},{6,4},{7,5},{8,10},{9,11},{10,... | collective-permute-start | bytes 10321928 | tf_op jit(solution)/shard_map/ppermute | solution.py:202
  776.9 113.3 %collective-permute-start.9 = (bf16[192,4480]{1,0:T(8,128)(2,1)}, bf16[192,4480]{1,0:T(8,128)(2,1)}, u32[]{:S(2)}, u32[]{:S(2)}) collective-permute-start(bf16[192,4480]{1,0:T(8,128)(2,1)} %fusion.59), channel_id=1, source_target_pairs={{0,2},{1,3},{2,0},{3,1},{4,6},{5,7},{6,4},{7,5},{8,10},{9,11},{10,... | collective-permute-start | bytes 5160968 | tf_op jit(solution)/shard_map/ppermute | solution.py:202
  777.8 113.6 %collective-permute-start.8 = (bf16[192,4480]{1,0:T(8,128)(2,1)S(1)}, bf16[192,4480]{1,0:T(8,128)(2,1)}, u32[]{:S(2)}, u32[]{:S(2)}) collective-permute-start(bf16[192,4480]{1,0:T(8,128)(2,1)S(1)} %fusion.58), channel_id=1, source_target_pairs={{0,4},{1,5},{2,6},{3,7},{4,0},{5,1},{6,2},{7,3},{8,12},{9,13},{10,... | collective-permute-start | bytes 5160968 | tf_op jit(solution)/shard_map/ppermute | solution.py:202
  792.7 171.2 %collective-permute-start.11 = (bf16[1120,1536]{1,0:T(8,128)(2,1)}, bf16[1120,1536]{1,0:T(8,128)(2,1)}, u32[]{:S(2)}, u32[]{:S(2)}) collective-permute-start(bf16[1120,1536]{1,0:T(8,128)(2,1)} %get-tuple-element.312), channel_id=1, source_target_pairs={{0,2},{1,3},{2,0},{3,1},{4,6},{5,7},{6,4},{7,5},{8,10},{9,11},{10,... | collective-permute-start | bytes 10321928 | tf_op jit(solution)/shard_map/ppermute | solution.py:202
  841.9 169.6 %collective-permute-start.12 = (bf16[384,4480]{1,0:T(8,128)(2,1)}, bf16[384,4480]{1,0:T(8,128)(2,1)}, u32[]{:S(2)}, u32[]{:S(2)}) collective-permute-start(bf16[384,4480]{1,0:T(8,128)(2,1)} %slice.276), channel_id=1, source_target_pairs={{0,4},{1,5},{2,6},{3,7},{4,0},{5,1},{6,2},{7,3},{8,12},{9,13},{10,... | collective-permute-start | bytes 10321928 | tf_op jit(solution)/shard_map/ppermute | solution.py:202
  890.2 148.4 %collective-permute-start.13 = (bf16[384,4480]{1,0:T(8,128)(2,1)}, bf16[384,4480]{1,0:T(8,128)(2,1)}, u32[]{:S(2)}, u32[]{:S(2)}) collective-permute-start(bf16[384,4480]{1,0:T(8,128)(2,1)} %slice.277), channel_id=1, source_target_pairs={{0,2},{1,3},{2,0},{3,1},{4,6},{5,7},{6,4},{7,5},{8,10},{9,11},{10,... | collective-permute-start | bytes 10321928 | tf_op jit(solution)/shard_map/ppermute | solution.py:202
  899.2 350.7 %collective-permute-start.33 = (bf16[192,4480]{1,0:T(8,128)(2,1)}, bf16[192,4480]{1,0:T(8,128)(2,1)}, u32[]{:S(2)}, u32[]{:S(2)}) collective-permute-start(bf16[192,4480]{1,0:T(8,128)(2,1)} %fusion.40), channel_id=1, source_target_pairs={{0,8},{8,0},{1,9},{9,1},{2,10},{10,2},{3,11},{11,3},{4,12},{12,4},... | collective-permute-start | bytes 5160968 | tf_op jit(solution)/shard_map/ppermute | solution.py:206
  1024.8 74.4 %collective-permute-start.19 = (bf16[192,4480]{1,0:T(8,128)(2,1)}, bf16[192,4480]{1,0:T(8,128)(2,1)}, u32[]{:S(2)}, u32[]{:S(2)}) collective-permute-start(bf16[192,4480]{1,0:T(8,128)(2,1)} %fusion.60), channel_id=1, source_target_pairs={{0,2},{1,3},{2,0},{3,1},{4,6},{5,7},{6,4},{7,5},{8,10},{9,11},{10,... | collective-permute-start | bytes 5160968 | tf_op jit(solution)/shard_map/ppermute | solution.py:202
  1038.6 90.9 %collective-permute-start.18 = (bf16[1120,1536]{1,0:T(8,128)(2,1)S(1)}, bf16[1120,1536]{1,0:T(8,128)(2,1)}, u32[]{:S(2)}, u32[]{:S(2)}) collective-permute-start(bf16[1120,1536]{1,0:T(8,128)(2,1)S(1)} %copy-done.35), channel_id=1, source_target_pairs={{0,4},{1,5},{2,6},{3,7},{4,0},{5,1},{6,2},{7,3},{8,12},{9,13},{10,... | collective-permute-start | bytes 10321928 | tf_op jit(solution)/shard_map/ppermute | solution.py:202
  1054.1 73.7 %collective-permute-start.17 = (bf16[384,768]{1,0:T(8,128)(2,1)S(1)}, bf16[384,768]{1,0:T(8,128)(2,1)S(1)}, u32[]{:S(2)}, u32[]{:S(2)}) collective-permute-start(bf16[384,768]{1,0:T(8,128)(2,1)S(1)} %slice.282), channel_id=1, source_target_pairs={{0,4},{1,5},{2,6},{3,7},{4,0},{5,1},{6,2},{7,3},{8,12},{9,13},{10,... | collective-permute-start | bytes 1769480 | tf_op jit(solution)/shard_map/ppermute | solution.py:202
  1054.3 75.3 %collective-permute-start.16 = (bf16[384,768]{1,0:T(8,128)(2,1)S(1)}, bf16[384,768]{1,0:T(8,128)(2,1)}, u32[]{:S(2)}, u32[]{:S(2)}) collective-permute-start(bf16[384,768]{1,0:T(8,128)(2,1)S(1)} %slice.283), channel_id=1, source_target_pairs={{0,2},{1,3},{2,0},{3,1},{4,6},{5,7},{6,4},{7,5},{8,10},{9,11},{10,... | collective-permute-start | bytes 1769480 | tf_op jit(solution)/shard_map/ppermute | solution.py:202
  1099.2 151.2 %collective-permute-start.31 = (bf16[192,4480]{1,0:T(8,128)(2,1)}, bf16[192,4480]{1,0:T(8,128)(2,1)}, u32[]{:S(2)}, u32[]{:S(2)}) collective-permute-start(bf16[192,4480]{1,0:T(8,128)(2,1)} %fusion.41), channel_id=1, source_target_pairs={{0,8},{8,0},{1,9},{9,1},{2,10},{10,2},{3,11},{11,3},{4,12},{12,4},... | collective-permute-start | bytes 5160968 | tf_op jit(solution)/shard_map/ppermute | solution.py:206
  1127.8 62.6 %collective-permute-start.20 = (bf16[192,4480]{1,0:T(8,128)(2,1)}, bf16[192,4480]{1,0:T(8,128)(2,1)}, u32[]{:S(2)}, u32[]{:S(2)}) collective-permute-start(bf16[192,4480]{1,0:T(8,128)(2,1)} %fusion.61), channel_id=1, source_target_pairs={{0,4},{1,5},{2,6},{3,7},{4,0},{5,1},{6,2},{7,3},{8,12},{9,13},{10,... | collective-permute-start | bytes 5160968 | tf_op jit(solution)/shard_map/ppermute | solution.py:202
  1135.7 56.2 %collective-permute-start.22 = (bf16[192,768]{1,0:T(8,128)(2,1)}, bf16[192,768]{1,0:T(8,128)(2,1)S(1)}, u32[]{:S(2)}, u32[]{:S(2)}) collective-permute-start(bf16[192,768]{1,0:T(8,128)(2,1)} %fusion.89), channel_id=1, source_target_pairs={{0,2},{1,3},{2,0},{3,1},{4,6},{5,7},{6,4},{7,5},{8,10},{9,11},{10,... | collective-permute-start | bytes 884744 | tf_op jit(solution)/shard_map/ppermute | solution.py:202
  1138.3 53.6 %collective-permute-start.21 = (bf16[192,768]{1,0:T(8,128)(2,1)}, bf16[192,768]{1,0:T(8,128)(2,1)}, u32[]{:S(2)}, u32[]{:S(2)}) collective-permute-start(bf16[192,768]{1,0:T(8,128)(2,1)} %fusion.88), channel_id=1, source_target_pairs={{0,4},{1,5},{2,6},{3,7},{4,0},{5,1},{6,2},{7,3},{8,12},{9,13},{10,... | collective-permute-start | bytes 884744 | tf_op jit(solution)/shard_map/ppermute | solution.py:202
  1190.4 166.8 %collective-permute-start.37 = (bf16[1120,1536]{1,0:T(8,128)(2,1)}, bf16[1120,1536]{1,0:T(8,128)(2,1)}, u32[]{:S(2)}, u32[]{:S(2)}) collective-permute-start(bf16[1120,1536]{1,0:T(8,128)(2,1)} %add_convert_fusion.1), channel_id=1, source_target_pairs={{0,8},{8,0},{1,9},{9,1},{2,10},{10,2},{3,11},{11,3},{4,12},{12,4},... | collective-permute-start | bytes 10321928 | tf_op jit(solution)/shard_map/ppermute | solution.py:206
  1240.1 117.2 %collective-permute-start.34 = (bf16[192,4480]{1,0:T(8,128)(2,1)}, bf16[192,4480]{1,0:T(8,128)(2,1)}, u32[]{:S(2)}, u32[]{:S(2)}) collective-permute-start(bf16[192,4480]{1,0:T(8,128)(2,1)} %fusion.39), channel_id=1, source_target_pairs={{0,8},{8,0},{1,9},{9,1},{2,10},{10,2},{3,11},{11,3},{4,12},{12,4},... | collective-permute-start | bytes 5160968 | tf_op jit(solution)/shard_map/ppermute | solution.py:206
  1241.2 116.0 %collective-permute-start.32 = (bf16[192,4480]{1,0:T(8,128)(2,1)}, bf16[192,4480]{1,0:T(8,128)(2,1)}, u32[]{:S(2)}, u32[]{:S(2)}) collective-permute-start(bf16[192,4480]{1,0:T(8,128)(2,1)} %fusion.38), channel_id=1, source_target_pairs={{0,8},{8,0},{1,9},{9,1},{2,10},{10,2},{3,11},{11,3},{4,12},{12,4},... | collective-permute-start | bytes 5160968 | tf_op jit(solution)/shard_map/ppermute | solution.py:206
  1265.4 83.5 %collective-permute-start.36 = (bf16[192,768]{1,0:T(8,128)(2,1)}, bf16[192,768]{1,0:T(8,128)(2,1)S(1)}, u32[]{:S(2)}, u32[]{:S(2)}) collective-permute-start(bf16[192,768]{1,0:T(8,128)(2,1)} %fusion.84), channel_id=1, source_target_pairs={{0,8},{8,0},{1,9},{9,1},{2,10},{10,2},{3,11},{11,3},{4,12},{12,4},... | collective-permute-start | bytes 884744 | tf_op jit(solution)/shard_map/ppermute | solution.py:206
  1266.1 89.0 %collective-permute-start.35 = (bf16[192,768]{1,0:T(8,128)(2,1)}, bf16[192,768]{1,0:T(8,128)(2,1)S(1)}, u32[]{:S(2)}, u32[]{:S(2)}) collective-permute-start(bf16[192,768]{1,0:T(8,128)(2,1)} %fusion.85), channel_id=1, source_target_pairs={{0,8},{8,0},{1,9},{9,1},{2,10},{10,2},{3,11},{11,3},{4,12},{12,4},... | collective-permute-start | bytes 884744 | tf_op jit(solution)/shard_map/ppermute | solution.py:206
  (117 other events, 1752.0 us)
Sparse Core Ops, SparseCore 0:
  10.4 44.6 all-gather.8
  57.0 35.0 all-gather.10
  93.9 73.2 all-gather.14
  168.9 73.2 all-gather.16
  243.9 131.4 all-gather.12
  377.0 74.1 all-gather.18
  453.0 73.2 all-gather.20
  1229.4 61.7 all-reduce.13
